TPU v7x, 8 devices: a whole 2x2x1 slice. The times are simulated.
8 devices in a mesh: replica: 1 (over z), model: 8 (over y, x, core).
Axes of the slice: x: 2, y: 2, z: 1, core: 2. Of those that a mesh axis runs over, the one named last changes fastest.
Arguments:
- tokens: bfloat16 [256, 6144], P('replica')
- lengths: int32 [256], P('replica')
- k_cache: bfloat16 [256, 1, 4096, 128], P('replica')
- v_cache: bfloat16 [256, 1, 4096, 128], P('replica')
- norm_gain: bfloat16 [6144], replicated
- w_query: bfloat16 [6144, 6144], P(None, 'model')
- w_key: bfloat16 [6144, 128], replicated
- w_value: bfloat16 [6144, 128], replicated
- w_out: bfloat16 [6144, 6144], P('model')
- w_gate: bfloat16 [6144, 24576], P(None, 'model')
- w_up: bfloat16 [6144, 24576], P(None, 'model')
- w_down: bfloat16 [24576, 6144], P('model')
Outputs:
- output 1: bfloat16 [256, 6144], P('replica')
- output 2: bfloat16 [256, 1, 128], P(('replica', 'model'))
- output 3: bfloat16 [256, 1, 128], P(('replica', 'model'))
All inputs are finite; a program needn't handle non-finite values.
Results may differ from a plain program's by a relative error of at most 0.00437682.
Values are sent between devices in bfloat16 or wider.
A program may use at most 2.75 GiB of HBM per device.

v0:
```python
import math
import jax
import jax.numpy as jnp
from jax import lax
from jax.sharding import PartitionSpec as P

ROPE_BASE = 10000.0
NORM_EPS = 1e-6
MASK_VALUE = -1e30


def rms_norm(tokens, norm_gain):
    values = tokens.astype(jnp.float32)
    mean_sq = jnp.mean(values * values, axis=-1, keepdims=True)
    return (values * lax.rsqrt(mean_sq + NORM_EPS) * norm_gain.astype(jnp.float32)).astype(jnp.bfloat16)


def apply_rope(values, positions):
    half_dim = values.shape[-1] // 2
    inv_freq = jnp.exp(jnp.arange(half_dim, dtype=jnp.float32) * (-2.0 * math.log(ROPE_BASE) / values.shape[-1]))
    angles = positions.astype(jnp.float32)[:, None, None] * inv_freq[None, None, :]
    cos_part = jnp.cos(angles)
    sin_part = jnp.sin(angles)
    first_half = values[..., :half_dim]
    second_half = values[..., half_dim:]
    return jnp.concatenate([first_half * cos_part - second_half * sin_part, second_half * cos_part + first_half * sin_part], axis=-1)


def attend(queries, key_rows, value_rows, key_new, value_new, row_lengths):
    row_count, heads, head_dim = queries.shape
    kv_heads = key_rows.shape[1]
    grouped = queries.reshape(row_count, kv_heads, heads // kv_heads, head_dim)
    scale = head_dim ** -0.5
    scores = jnp.einsum('bgrd,bgtd->bgrt', grouped, key_rows, preferred_element_type=jnp.float32) * scale
    valid = jnp.arange(key_rows.shape[2])[None, None, None, :] < row_lengths[:, None, None, None]
    scores = jnp.where(valid, scores, MASK_VALUE)
    score_new = jnp.einsum('bgrd,bgd->bgr', grouped, key_new, preferred_element_type=jnp.float32) * scale
    peak = jnp.maximum(jnp.max(scores, axis=-1), score_new)
    weights = jnp.exp(scores - peak[..., None])
    weight_new = jnp.exp(score_new - peak)
    total = jnp.sum(weights, axis=-1) + weight_new
    mixed = jnp.einsum('bgrt,bgtd->bgrd', weights.astype(jnp.bfloat16), value_rows, preferred_element_type=jnp.float32)
    mixed = mixed + weight_new.astype(jnp.bfloat16).astype(jnp.float32)[..., None] * value_new.astype(jnp.float32)[:, :, None, :]
    return (mixed / total[..., None]).astype(jnp.bfloat16).reshape(row_count, heads, head_dim)


def solution(mesh):
    groups = mesh.shape['model']

    def local_step(tokens, lengths, k_cache, v_cache, norm_gain, w_query, w_key, w_value, w_out, w_gate, w_up, w_down):
        batch = tokens.shape[0]
        kv_heads = k_cache.shape[1]
        head_dim = k_cache.shape[3]
        local_heads = w_query.shape[1] // head_dim
        row_count = batch // groups
        row_start = lax.axis_index('model') * row_count
        normed = rms_norm(tokens, norm_gain)
        queries = apply_rope(jnp.dot(normed, w_query, preferred_element_type=jnp.float32).reshape(batch, local_heads, head_dim), lengths).astype(jnp.bfloat16)
        queries = lax.all_to_all(queries, 'model', 0, 1, tiled=True)
        row_lengths = lax.dynamic_slice_in_dim(lengths, row_start, row_count)
        row_normed = lax.dynamic_slice_in_dim(normed, row_start, row_count)
        key_new = apply_rope(jnp.dot(row_normed, w_key, preferred_element_type=jnp.float32).reshape(row_count, kv_heads, head_dim), row_lengths).astype(jnp.bfloat16)
        value_new = jnp.dot(row_normed, w_value, preferred_element_type=jnp.float32).reshape(row_count, kv_heads, head_dim).astype(jnp.bfloat16)
        key_rows = lax.dynamic_slice_in_dim(k_cache, row_start, row_count)
        value_rows = lax.dynamic_slice_in_dim(v_cache, row_start, row_count)
        attended = attend(queries, key_rows, value_rows, key_new, value_new, row_lengths)
        attended = lax.all_to_all(attended, 'model', 1, 0, tiled=True)
        hidden = (jax.nn.silu(jnp.dot(normed, w_gate, preferred_element_type=jnp.float32)) * jnp.dot(normed, w_up, preferred_element_type=jnp.float32)).astype(jnp.bfloat16)
        partial_sum = jnp.dot(attended.reshape(batch, local_heads * head_dim), w_out, preferred_element_type=jnp.float32) + jnp.dot(hidden, w_down, preferred_element_type=jnp.float32)
        summed = lax.psum(partial_sum, 'model')
        return (tokens.astype(jnp.float32) + summed).astype(jnp.bfloat16), key_new, value_new

    in_specs = (P('replica', None), P('replica'), P('replica', None, None, None), P('replica', None, None, None), P(None), P(None, 'model'), P(None, None), P(None, None), P('model', None), P(None, 'model'), P(None, 'model'), P('model', None))
    out_specs = (P('replica', None), P(('replica', 'model'), None, None), P(('replica', 'model'), None, None))
    return jax.shard_map(local_step, mesh=mesh, in_specs=in_specs, out_specs=out_specs, check_vma=False)
```

profile of v0, /device:TPU:0, one launch (start us, length us, event | category | flops | bytes accessed | tf_op | source)
XLA Modules:
  0.0 263.4 jit_solution(9068684658974445599)
XLA Ops:
  7.2 0.0 copy-start
  7.2 0.0 copy-start.4
  7.2 0.8 convert_element_type.62
  8.0 2.8 %fusion.14 = f32[256]{0:T(256)S(1)} fusion(bf16[256,6144]{1,0:T(8,128)(2,1)} %param.12), kind=kLoop, calls=%fused_computation.19 | loop fusion | flops 4718336 | bytes 3146752 | tf_op jit(solution)/shard_map/reduce_sum | solution.py:14
  10.9 0.8 convert_element_type.60
  11.7 0.3 multiply_cosine_fusion
  12.0 2.8 %fusion.16 = bf16[256,6144]{1,0:T(8,128)(2,1)S(1)} fusion(bf16[256,6144]{1,0:T(8,128)(2,1)} %param.12, f32[6144]{0:T(1024)S(1)} %convert_element_type.60, f32[256]{0:T(256)S(1)} %add_rsqrt_fusion), kind=kLoop, calls=%fused_computation.21 | loop fusion | flops 6291456 | bytes 6317056 | tf_op jit(solution)/shard_map/convert_element_type | solution.py:15
  14.8 0.0 copy-done.4
  14.8 0.0 copy-start.2
  14.8 0.0 copy-start.3
  14.8 4.0 %fusion.66 = f32[256,768]{0,1:T(8,128)S(1)} fusion(bf16[256,6144]{1,0:T(8,128)(2,1)S(1)} %fusion.16, bf16[6144,768]{1,0:T(8,128)(2,1)S(1)} %copy-done.4), kind=kOutput, calls=%fused_computation.77 | convolution fusion | flops 2415919104 | bytes 13369344 | tf_op jit(solution)/shard_map/dot_general | solution.py:58
  18.8 0.0 copy-done.2
  18.8 0.1 subtract_convert_fusion
  18.9 1.1 copy.28
  20.0 4.3 %all-to-all-start = ((bf16[256,6,128]{2,1,0:T(8,128)(2,1)}), bf16[256,6,128]{2,1,0:T(8,128)(2,1)S(1)}, u32[]{:S(2)}, u32[]{:S(2)}) async-start(bf16[256,6,128]{2,1,0:T(8,128)(2,1)} %copy.28), calls=%async_computation | async-start | bytes 1048576 | tf_op jit(solution)/shard_map/all_to_all | solution.py:59
  24.3 0.0 copy-done.3
  24.3 0.1 fusion.64
  24.4 0.1 iota_compare_fusion
  24.5 1.9 convolution_bitcast_fusion
  26.5 18.9 %fusion.67 = f32[256,3072]{1,0:T(8,128)} fusion(bf16[256,6144]{1,0:T(8,128)(2,1)} %copy-done.2, bf16[6144,3072]{1,0:T(8,128)(2,1)} %param.21), kind=kOutput, calls=%fused_computation.78 | convolution fusion | flops 9663676416 | bytes 44040192 | tf_op jit(solution)/shard_map/dot_general | solution.py:68
  45.4 0.1 fusion.52
  45.5 0.1 maximum_bitcast_fusion
  45.6 0.0 copy-done
  45.6 2.0 fusion.65
  47.6 0.0 all-to-all-done
  47.6 0.1 copy.30
  47.6 0.3 fusion.42
  47.9 23.2 %fusion.6 = (f32[32,48]{1,0:T(8,128)S(1)}, f32[32,48,4096]{2,1,0:T(8,128)}) fusion(pred[32,4096]{1,0:T(8,128)(4,1)S(1)} %iota_compare_fusion, bf16[256,1,4096,128]{3,2,1,0:T(8,128)(2,1)} %param.14, s32[]{:T(128)S(6)} %select_n.11, bf16[32,48,128]{2,0,1:T(8,128)(2,1)S(1)} %bitcast.56), kind=kOutput, calls=%fused_computation.8 | convolution fusion | flops 1629485568 | bytes 59250692 | tf_op jit(solution)/shard_map/bgrd,bgtd->bgrt/dot_general | solution.py:34
  71.1 11.5 %fusion.7 = f32[32,48]{1,0:T(8,128)S(1)} fusion(f32[32,48,4096]{2,1,0:T(8,128)} %get-tuple-element.14, f32[32,48]{1,0:T(8,128)S(1)} %multiply_maximum_fusion, pred[32,4096]{1,0:T(8,128)(4,1)S(1)} %iota_compare_fusion), kind=kLoop, calls=%fused_computation.9 | loop fusion | flops 25164288 | bytes 25309184 | tf_op jit(solution)/shard_map/reduce_sum | solution.py:41
  82.7 20.8 %fusion.34 = bf16[32,48,128]{2,1,0:T(8,128)(2,1)S(1)} fusion(bf16[256,1,4096,128]{3,2,1,0:T(8,128)(2,1)} %param.15, s32[]{:T(128)S(6)} %select_n.11, f32[32,48,4096]{2,1,0:T(8,128)} %get-tuple-element.14, f32[32,48]{1,0:T(8,128)S(1)} %multiply_maximum_fusion, pred[32,4096]{1,0:T(8,128)(4,1)S(1)} %iota_compare_fusion, f32[32,48]{1,0:T(8,128)S(1)} %get-tuple-element.8, ...), kind=kOutput, calls=%fused_computation.34 | convolution fusion | flops 1636564992 | bytes 59279364 | tf_op jit(solution)/shard_map/bgrt,bgtd->bgrd/dot_general | solution.py:42
  103.5 0.9 copy.32
  104.3 2.9 %all-to-all-start.1 = ((bf16[32,48,128]{2,0,1:T(8,128)(2,1)}), bf16[32,48,128]{2,0,1:T(8,128)(2,1)S(1)}, u32[]{:S(2)}, u32[]{:S(2)}) async-start(bf16[32,48,128]{2,0,1:T(8,128)(2,1)} %copy.32), calls=%async_computation.1 | async-start | bytes 786432 | tf_op jit(solution)/shard_map/all_to_all | solution.py:67
  107.2 0.3 all-reduce.2.cloned.1.call-start
  107.5 19.5 %fusion.18.clone.4 = bf16[256,3072]{1,0:T(8,128)(2,1)} fusion(bf16[256,6144]{1,0:T(8,128)(2,1)} %copy-done.2, bf16[6144,3072]{1,0:T(8,128)(2,1)} %param.22, f32[256,3072]{1,0:T(8,128)} %fusion.67), kind=kOutput, calls=%fused_computation.24.clone.clone.clone.1 | convolution fusion | flops 9668395008 | bytes 45613056 | tf_op jit(solution)/shard_map/dot_general | solution.py:68
  127.0 0.0 all-to-all-done.1
  127.0 0.2 copy.33
  127.2 8.2 %fusion.39 = f32[256,6144]{1,0:T(8,128)} fusion(bf16[768,6144]{1,0:T(8,128)(2,1)} %param.20, bf16[32,8,6,128]{3,2,1,0:T(8,128)(2,1)S(1)} %bitcast.57), kind=kOutput, calls=%fused_computation.36 | convolution fusion | flops 2415919104 | bytes 16121856 | tf_op jit(solution)/shard_map/dot_general | solution.py:69
  135.3 21.3 %convolution_add_fusion = f32[256,6144]{1,0:T(8,128)} fusion(f32[256,6144]{1,0:T(8,128)} %fusion.39, bf16[3072,6144]{1,0:T(8,128)(2,1)} %param.23, bf16[256,3072]{1,0:T(8,128)(2,1)} %fusion.18.clone.4), kind=kOutput, calls=%fused_computation.18 | convolution fusion | flops 9665249280 | bytes 51904512 | tf_op jit(solution)/shard_map/dot_general | solution.py:69
  156.6 0.0 all-reduce.2.cloned.1.call-update
  156.6 0.0 copy-start.1
  156.7 0.7 pad_maximum_fusion.1
  157.3 93.0 %all-reduce.2.cloned.1.call-done = f32[256,6144]{1,0:T(8,128)} async-done(((f32[256,6144]{1,0:T(8,128)}), f32[256,6144]{1,0:T(8,128)}) %all-reduce.2.cloned.1.call-update) | async-done | bytes 6291472 | tf_op jit(solution)/shard_map/psum | solution.py:70
  250.4 6.2 %fusion.17 = bf16[256,6144]{1,0:T(8,128)(2,1)} fusion(f32[256,6144]{1,0:T(8,128)} %all-reduce.2.cloned.1.call-done, bf16[256,6144]{1,0:T(8,128)(2,1)} %param.12), kind=kLoop, calls=%fused_computation.22 | loop fusion | flops 4718592 | bytes 12582912 | tf_op jit(solution)/shard_map/convert_element_type | solution.py:71
  256.6 0.0 copy-done.1
  (5 shorter events, 0.1 us)
Async XLA Ops:
  7.2 38.4 %copy-start = (bf16[6144,128]{1,0:T(8,128)(2,1)S(1)}, bf16[6144,128]{1,0:T(8,128)(2,1)}, u32[]{:S(2)}) copy-start(bf16[6144,128]{1,0:T(8,128)(2,1)} %param.19) | copy-start | bytes 4718596
  7.2 7.6 %copy-start.4 = (bf16[6144,768]{1,0:T(8,128)(2,1)S(1)}, bf16[6144,768]{1,0:T(8,128)(2,1)}, u32[]{:S(2)}) copy-start(bf16[6144,768]{1,0:T(8,128)(2,1)} %param.17) | copy-start | bytes 28311556
  14.8 4.0 %copy-start.2 = (bf16[256,6144]{1,0:T(8,128)(2,1)}, bf16[256,6144]{1,0:T(8,128)(2,1)S(1)}, u32[]{:S(2)}) copy-start(bf16[256,6144]{1,0:T(8,128)(2,1)S(1)} %fusion.16) | copy-start | bytes 9437188
  14.8 9.5 %copy-start.3 = (s32[256]{0:T(256)S(1)}, s32[256]{0:T(256)}, u32[]{:S(2)}) copy-start(s32[256]{0:T(256)} %param.13) | copy-start | bytes 3076
  20.0 27.6 %all-to-all-start = ((bf16[256,6,128]{2,1,0:T(8,128)(2,1)}), bf16[256,6,128]{2,1,0:T(8,128)(2,1)S(1)}, u32[]{:S(2)}, u32[]{:S(2)}) async-start(bf16[256,6,128]{2,1,0:T(8,128)(2,1)} %copy.28), calls=%async_computation | async-start | bytes 1048576 | tf_op jit(solution)/shard_map/all_to_all | solution.py:59
  104.3 22.7 %all-to-all-start.1 = ((bf16[32,48,128]{2,0,1:T(8,128)(2,1)}), bf16[32,48,128]{2,0,1:T(8,128)(2,1)S(1)}, u32[]{:S(2)}, u32[]{:S(2)}) async-start(bf16[32,48,128]{2,0,1:T(8,128)(2,1)} %copy.32), calls=%async_computation.1 | async-start | bytes 786432 | tf_op jit(solution)/shard_map/all_to_all | solution.py:67
  107.2 143.1 %all-reduce.2.cloned.1.call-start = ((), (), s32[]{:S(2)}) async-start(), calls=%async_computation.2 | async-start | bytes 12582912 | tf_op jit(solution)/shard_map/psum | solution.py:70
  156.6 99.9 %copy-start.1 = (bf16[6144,128]{1,0:T(8,128)(2,1)S(1)}, bf16[6144,128]{1,0:T(8,128)(2,1)}, u32[]{:S(2)}) copy-start(bf16[6144,128]{1,0:T(8,128)(2,1)} %param.19) | copy-start | bytes 4718596
Sparse Core Ops, SparseCore 0:
  156.8 93.5 all-reduce.1
where the time goes:
time: 264 us; the launch traced here: 263 us
  matrix products  120 us (45%)
  waiting for transfers between devices  93 us (35%)
  other arithmetic  26.5 us (10%)
  between operations  14.2 us (5%)
  starting transfers between devices  7.49 us (3%)
    psum x1, waiting for transfers between devices, local_step(): summed = lax.psum(partial_sum, 'model')  93 us
    dot_general x1, matrix products, attend(): jnp.einsum('bgrd,bgtd->bgrt', grouped, key_rows, preferred_element_type=j...  23.2 us
    dot_general x1, matrix products, local_step(): jnp.dot(hidden, w_down, preferred_element_type=jnp.float32)  21.3 us
    dot_general x1, matrix products, attend(): jnp.einsum('bgrt,bgtd->bgrd', weights.astype(jnp.bfloat16), value_rows, p...  20.8 us
    dot_general x1, matrix products, local_step(): jnp.dot(normed, w_up, preferred_element_type=jnp.float32)  19.5 us
    dot_general x1, matrix products, local_step(): jnp.dot(normed, w_gate, preferred_element_type=jnp.float32)  18.9 us
    reduce_sum x1, other arithmetic, attend(): total = jnp.sum(weights, axis=-1) + weight_new  11.5 us
    dot_general x1, matrix products, local_step(): jnp.dot(attended.reshape(batch, local_heads * head_dim), w_out, preferred...  8.16 us
  transfers between devices with their start and end apart: 3, of which 1 were waited for; matrix products, arithmetic and copies ran while one was open for 16% of the time, Pallas kernels for 0%

commit v1 on v0

v1 whole, which is shorter than its diff:
```python
import functools
import math
import jax
import jax.numpy as jnp
from jax import lax
from jax.experimental import pallas as pl
from jax.experimental.pallas import tpu as pltpu
from jax.sharding import PartitionSpec as P

ROPE_BASE = 10000.0
NORM_EPS = 1e-6
MASK_VALUE = -1e30
BF16, F32 = jnp.bfloat16, jnp.float32
MESH = pl.DeviceIdType.MESH

PEERS = 8
SLOTS = 3
BLOCK = 512
EARLY = 5
CHUNK = 512
ITEMS = 4
RING = 4
LAGS = (0, 1, 2, 3, 4, 5, 6)


def greet(me):
    barrier = pltpu.get_barrier_semaphore()
    for step in range(1, PEERS):
        peer = lax.rem(me + step, PEERS)
        pl.semaphore_signal(barrier, inc=1, device_id={"model": peer}, device_id_type=MESH)
    return barrier


def gate_up_copies(block, slot, gate_hbm, up_hbm, ring, sems):
    half = BLOCK // 2
    columns = pl.ds(pl.multiple_of(block * half, half), half)
    return (
        pltpu.make_async_copy(gate_hbm.at[:, columns], ring.at[slot, :, pl.ds(0, half)], sems.at[slot, 0]),
        pltpu.make_async_copy(up_hbm.at[:, columns], ring.at[slot, :, pl.ds(half, half)], sems.at[slot, 1]),
    )


def hidden_block(normed, weights):
    half = BLOCK // 2
    both = jnp.dot(normed, weights, preferred_element_type=F32)
    gate, up = both[:, :half], both[:, half:]
    return (gate * lax.logistic(gate) * up).astype(BF16)


def rope(values, cos_part, sin_part):
    return values * cos_part + pltpu.roll(values, 64, 1) * sin_part


def project_kernel(x_hbm, lengths_ref, gain_ref, wq_hbm, wk_hbm, wv_hbm, gate_hbm, up_hbm,
                   q_out, knew_ref, vnew_ref, normed_hbm, hidden_ref,
                   x_ref, normed, ring, q_scr, cos_scr, sin_scr, x_sem, sems, n_sem, send_sem, recv_sem):
    me = lax.axis_index("model")
    batch = x_ref.shape[0]
    rows = batch // PEERS
    barrier = greet(me)
    x_copy = pltpu.make_async_copy(x_hbm, x_ref, x_sem)
    x_copy.start()
    first = (pltpu.make_async_copy(wq_hbm.at[:, pl.ds(0, 512)], ring.at[0], sems.at[0, 0]),)
    second = (
        pltpu.make_async_copy(wq_hbm.at[:, pl.ds(512, 256)], ring.at[1, :, pl.ds(0, 256)], sems.at[1, 0]),
        pltpu.make_async_copy(wk_hbm, ring.at[1, :, pl.ds(256, 128)], sems.at[1, 1]),
        pltpu.make_async_copy(wv_hbm, ring.at[1, :, pl.ds(384, 128)], sems.at[1, 2]),
    )
    gu = lambda block, slot: gate_up_copies(block, slot, gate_hbm, up_hbm, ring, sems)
    for copy in first + second + gu(0, 2):
        copy.start()

    lane = lax.broadcasted_iota(jnp.int32, (batch, 128), 1)
    pair = jnp.where(lane < 64, lane, lane - 64).astype(F32)
    inv_freq = jnp.exp(pair * (-2.0 * math.log(ROPE_BASE) / 128))
    angles = lengths_ref[...].astype(F32) * inv_freq
    cos_scr[...] = jnp.cos(angles)
    sin_scr[...] = jnp.where(lane < 64, -jnp.sin(angles), jnp.sin(angles))

    x_copy.wait()

    def norm_rows(r, _):
        at = pl.ds(pl.multiple_of(r * 16, 16), 16)
        values = x_ref[at, :].astype(F32)
        mean_sq = jnp.mean(values * values, axis=-1, keepdims=True)
        normed[at, :] = (values * lax.rsqrt(mean_sq + NORM_EPS) * gain_ref[...].astype(F32)).astype(BF16)
        return 0

    lax.fori_loop(0, batch // 16, norm_rows, 0)
    n_copy = pltpu.make_async_copy(normed, normed_hbm, n_sem)
    n_copy.start()

    for copy in first:
        copy.wait()
    head4 = jnp.dot(normed[...], ring[0], preferred_element_type=F32)
    for h in range(4):
        q_scr[h] = rope(head4[:, h * 128:(h + 1) * 128], cos_scr[...], sin_scr[...]).astype(BF16)
    if EARLY > 1:
        for copy in gu(1, 0):
            copy.start()
    for copy in second:
        copy.wait()
    tail = jnp.dot(normed[...], ring[1], preferred_element_type=F32)
    for h in range(2):
        q_scr[4 + h] = rope(tail[:, h * 128:(h + 1) * 128], cos_scr[...], sin_scr[...]).astype(BF16)
    k_all = rope(tail[:, 256:384], cos_scr[...], sin_scr[...])
    cos_scr[...] = k_all
    sin_scr[...] = tail[:, 384:512]
    mine = pl.ds(pl.multiple_of(me * rows, rows), rows)
    knew_ref[...] = cos_scr[mine, :].astype(BF16)
    vnew_ref[...] = sin_scr[mine, :].astype(BF16)
    if EARLY > 2:
        for copy in gu(2, 1):
            copy.start()

    pl.semaphore_wait(barrier, PEERS - 1)
    heads = pl.ds(me * 6, 6)
    sends = []
    for step in range(1, PEERS):
        peer = lax.rem(me + step, PEERS)
        sends.append(pltpu.make_async_remote_copy(
            src_ref=q_scr.at[:, pl.ds(pl.multiple_of(peer * rows, rows), rows), :],
            dst_ref=q_out.at[heads],
            send_sem=send_sem.at[step], recv_sem=recv_sem.at[step],
            device_id={"model": peer}, device_id_type=MESH))
        sends[-1].start()
    q_out[heads] = q_scr[:, mine, :]

    half = BLOCK // 2

    def block_step(n, _):
        slot = lax.rem(n + 2, SLOTS)
        for copy in gu(n, slot):
            copy.wait()
        hidden_ref[:, pl.ds(pl.multiple_of(n * half, half), half)] = hidden_block(normed[...], ring[slot])

        @pl.when(n + 3 < EARLY)
        def _():
            for copy in gu(n + 3, slot):
                copy.start()
        return 0

    lax.fori_loop(0, EARLY, block_step, 0)
    for copy in sends:
        copy.wait()
    n_copy.wait()


def attend_kernel(lengths_ref, q_ref, knew_ref, vnew_ref, k_hbm, v_hbm, o_ref,
                  q_scr, o_scr, k_scr, v_scr, k_buf, v_buf, item_row, item_chunk, m_run, l_run, acc_run, k_sem, v_sem):
    me = lax.axis_index("model")
    rows = o_ref.shape[1]
    head_count = o_ref.shape[0]
    base = me * rows
    scale = 128 ** -0.5

    def list_row(b, count):
        chunks = lax.div(lengths_ref[base + b] + (CHUNK - 1), CHUNK)

        def put(c, _):
            item_row[count + c] = b
            item_chunk[count + c] = c
            return 0
        lax.fori_loop(0, chunks, put, 0)
        return count + chunks

    total = lax.fori_loop(0, rows, list_row, jnp.int32(0))
    for extra in range(ITEMS - 1):
        item_row[total + extra] = rows - 1
        item_chunk[total + extra] = 64
    bodies = lax.div(total + (ITEMS - 1), ITEMS)

    def pieces(g, act):
        for j in range(ITEMS):
            n = g * ITEMS + j
            slot = lax.rem(g, RING) * ITEMS + j

            @pl.when(n < total)
            def _():
                b = item_row[n]
                start = item_chunk[n] * CHUNK
                count = jnp.minimum(lax.div(lengths_ref[base + b] - start + 127, 128), CHUNK // 128)

                def piece(p, _):
                    src = pl.ds(pl.multiple_of(start + p * 128, 128), 128)
                    dst = pl.ds(pl.multiple_of(p * 128, 128), 128)
                    act(pltpu.make_async_copy(k_hbm.at[base + b, 0, src, :], k_buf.at[slot, dst, :], k_sem.at[slot]))
                    act(pltpu.make_async_copy(v_hbm.at[base + b, 0, src, :], v_buf.at[slot, dst, :], v_sem.at[slot]))
                    return 0
                lax.fori_loop(0, count, piece, 0)

    k_buf[...] = jnp.zeros_like(k_buf)
    v_buf[...] = jnp.zeros_like(v_buf)
    for g in range(RING - 1):
        pieces(g, lambda copy: copy.start())

    for h in range(head_count):
        q_scr[:, h, :] = q_ref[h].astype(F32)
    k_scr[...] = knew_ref[...].astype(F32)
    v_scr[...] = vnew_ref[...].astype(F32)
    m_run[...] = jnp.zeros_like(m_run)
    l_run[...] = jnp.ones_like(l_run)
    acc_run[...] = jnp.zeros_like(acc_run)

    def body(g, _):
        pieces(g + RING - 1, lambda copy: copy.start())
        pieces(g, lambda copy: copy.wait())
        m, l, acc = m_run[...], l_run[...], acc_run[...]
        scored = []
        for j in range(ITEMS):
            n = g * ITEMS + j
            slot = lax.rem(g, RING) * ITEMS + j
            b, c = item_row[n], item_chunk[n]
            left = lengths_ref[base + b] - c * CHUNK
            q32 = q_scr[b]
            s = lax.dot_general(q32.astype(BF16), k_buf[slot], (((1,), (1,)), ((), ())), preferred_element_type=F32) * scale
            s = jnp.where(lax.broadcasted_iota(jnp.int32, s.shape, 1) < left, s, MASK_VALUE)
            s_new = jnp.sum(q32 * k_scr[pl.ds(b, 1), :], axis=-1, keepdims=True) * scale
            scored.append((s, jnp.max(s, axis=-1, keepdims=True), s_new, b, c, slot))
        for s, s_max, s_new, b, c, slot in scored:
            first = c == 0
            m_prev = jnp.where(first, s_new, m)
            l_prev = jnp.where(first, 1.0, l)
            acc_prev = jnp.where(first, v_scr[pl.ds(b, 1), :], acc)
            m = jnp.maximum(m_prev, s_max)
            e = jnp.exp(s - m)
            shrink = jnp.exp(m_prev - m)
            l = l_prev * shrink + jnp.sum(e, axis=-1, keepdims=True)
            acc = acc_prev * shrink + jnp.dot(e.astype(BF16), v_buf[slot], preferred_element_type=F32)
            o_scr[b] = acc / l
        m_run[...], l_run[...], acc_run[...] = m, l, acc
        return 0

    lax.fori_loop(0, bodies, body, 0)
    for h in range(head_count):
        o_ref[h] = o_scr[:, h, :].astype(BF16)


def combine_kernel(o_ref, x_hbm, normed_hbm, early_hbm, gate_hbm, up_hbm, wo_hbm, wd_hbm, y_ref,
                   normed, act, ring, o_full, x_rows, part, pair_in, in1x, in1y, in2x, in2y,
                   n_sem, e_sem, x_sem, sems, o_send, o_recv, c_send, c_recv):
    me = lax.axis_index("model")
    core = lax.rem(me, 2)
    xi = lax.rem(lax.div(me, 2), 2)
    yi = lax.div(me, 4)
    partner = me + 1 - 2 * core
    x_peer = me + 2 - 4 * xi
    y_peer = me + 4 - 8 * yi
    batch = normed.shape[0]
    rows = batch // PEERS
    late = gate_hbm.shape[1] // (BLOCK // 2) - EARLY
    n_chunks = y_ref.shape[1] // BLOCK
    o_width = wo_hbm.shape[0]
    f_width = wd_hbm.shape[0]
    half = BLOCK // 2
    barrier = greet(me)

    n_copy = pltpu.make_async_copy(normed_hbm, normed, n_sem)
    n_copy.start()
    early_width = EARLY * half
    e_copy = pltpu.make_async_copy(early_hbm, act.at[:, pl.ds(o_width, early_width)], e_sem)

    def gu(n, slot):
        return gate_up_copies(n + EARLY, slot, gate_hbm, up_hbm, ring, sems)

    def down(t, slot):
        columns = pl.ds(pl.multiple_of(t * BLOCK, BLOCK), BLOCK)
        return (
            pltpu.make_async_copy(wo_hbm.at[:, columns], ring.at[slot, pl.ds(0, o_width), :], sems.at[slot, 0]),
            pltpu.make_async_copy(wd_hbm.at[:, columns], ring.at[slot, pl.ds(o_width, f_width), :], sems.at[slot, 1]),
        )

    def fetch(n):
        slot = lax.rem(n, SLOTS)

        @pl.when(n < late)
        def _():
            for copy in gu(n, slot):
                copy.start()

        @pl.when((n >= late) & (n < late + n_chunks))
        def _():
            for copy in down(n - late, slot):
                copy.start()

    for n in range(SLOTS):
        for copy in gu(n, n):
            copy.start()
    e_copy.start()
    row_x = core * 128 + xi * 32 + yi * 16
    row_y = core * 128 + 64 + yi * 32 + xi * 16
    x_copies = []
    for k, row in enumerate((row_x, row_y)):
        x_copies.append(pltpu.make_async_copy(x_hbm.at[pl.ds(pl.multiple_of(row, 16), 16), :], x_rows.at[k], x_sem.at[k]))
        x_copies[-1].start()
    pl.semaphore_wait(barrier, PEERS - 1)
    mine = pl.ds(pl.multiple_of(me * rows, rows), rows)
    sends = []
    for step in range(1, PEERS):
        peer = lax.rem(me + step, PEERS)
        sends.append(pltpu.make_async_remote_copy(
            src_ref=o_ref.at[pl.ds(peer * 6, 6)], dst_ref=o_full.at[:, mine, :],
            send_sem=o_send.at[step], recv_sem=o_recv.at[step],
            device_id={"model": peer}, device_id_type=MESH))
        sends[-1].start()
    o_full[:, mine, :] = o_ref[pl.ds(me * 6, 6)]
    n_copy.wait()

    def block_step(n, _):
        slot = lax.rem(n, SLOTS)
        for copy in gu(n, slot):
            copy.wait()
        at = pl.ds(pl.multiple_of(o_width + early_width + n * half, half), half)
        act[:, at] = hidden_block(normed[...], ring[slot])
        fetch(n + SLOTS)
        return 0

    lax.fori_loop(0, late, block_step, 0)
    e_copy.wait()
    for copy in x_copies:
        copy.wait()
    for copy in sends:
        copy.wait()
    for h in range(6):
        act[:, h * 128:(h + 1) * 128] = o_full[h]

    my_half = pl.multiple_of(core * 128, 128)
    other_half = pl.multiple_of(128 - core * 128, 128)
    keep1x = pl.multiple_of(my_half + xi * 32, 32)
    give1x = pl.multiple_of(my_half + 32 - xi * 32, 32)
    keep1y = pl.multiple_of(my_half + 64 + yi * 32, 32)
    give1y = pl.multiple_of(my_half + 96 - yi * 32, 32)
    keep2x = pl.multiple_of(keep1x + yi * 16, 16)
    give2x = pl.multiple_of(keep1x + 16 - yi * 16, 16)
    keep2y = pl.multiple_of(keep1y + xi * 16, 16)
    give2y = pl.multiple_of(keep1y + 16 - xi * 16, 16)

    def cols(t):
        return pl.ds(pl.multiple_of(t * BLOCK, BLOCK), BLOCK)

    def remote(kind, t, src, dst, peer):
        return pltpu.make_async_remote_copy(
            src_ref=src, dst_ref=dst, send_sem=c_send.at[kind, t], recv_sem=c_recv.at[kind, t],
            device_id={"model": peer}, device_id_type=MESH)

    def pair_sum(t):
        return remote(0, t, part.at[t, pl.ds(other_half, 128), :], pair_in.at[t], partner)

    def scatter1(t):
        return (remote(1, t, part.at[t, pl.ds(give1x, 32), :], in1x.at[t], x_peer),
                remote(2, t, part.at[t, pl.ds(give1y, 32), :], in1y.at[t], y_peer))

    def scatter2(t):
        return (remote(3, t, part.at[t, pl.ds(give2x, 16), :], in2x.at[t], y_peer),
                remote(4, t, part.at[t, pl.ds(give2y, 16), :], in2y.at[t], x_peer))

    def spread(kind, t, row, count, peer):
        at = y_ref.at[pl.ds(row, count), cols(t)]
        return remote(kind, t, at, at, peer)

    def gather1(t):
        return spread(5, t, keep2x, 16, y_peer), spread(6, t, keep2y, 16, x_peer)

    def gather2(t):
        return spread(7, t, keep1x, 32, x_peer), spread(8, t, keep1y, 32, y_peer)

    def pair_copy(t):
        return (spread(9, t, my_half, 128, partner),)

    def start(copies):
        for copy in copies:
            copy.start()

    def arrive(copies):
        for copy in copies:
            copy.wait_recv()

    def stage_compute(t):
        slot = lax.rem(t + late, SLOTS)
        for copy in down(t, slot):
            copy.wait()
        part[t] = jnp.dot(act[...], ring[slot, pl.ds(0, o_width + f_width), :], preferred_element_type=F32)
        pair_sum(t).start()
        fetch(t + late + SLOTS)

    def stage_scatter1(t):
        pair_sum(t).wait_recv()
        part[t, pl.ds(my_half, 128), :] = part[t, pl.ds(my_half, 128), :] + pair_in[t]
        start(scatter1(t))

    def stage_scatter2(t):
        arrive(scatter1(t))
        part[t, pl.ds(keep1x, 32), :] = part[t, pl.ds(keep1x, 32), :] + in1x[t]
        part[t, pl.ds(keep1y, 32), :] = part[t, pl.ds(keep1y, 32), :] + in1y[t]
        start(scatter2(t))

    def stage_gather1(t):
        arrive(scatter2(t))
        for k, (keep, inbox) in enumerate(((keep2x, in2x), (keep2y, in2y))):
            total = part[t, pl.ds(keep, 16), :] + inbox[t]
            y_ref[pl.ds(keep, 16), cols(t)] = (x_rows[k, :, cols(t)].astype(F32) + total).astype(BF16)
        start(gather1(t))

    def stage_gather2(t):
        arrive(gather1(t))
        start(gather2(t))

    def stage_pair(t):
        arrive(gather2(t))
        start(pair_copy(t))

    def stage_end(t):
        arrive(pair_copy(t))

    stages = (stage_compute, stage_scatter1, stage_scatter2, stage_gather1, stage_gather2, stage_pair, stage_end)

    def iteration(i, _):
        for lag, stage in zip(LAGS, stages):
            t = i - lag

            @pl.when((t >= 0) & (t < n_chunks))
            def _(stage=stage, t=t):
                stage(t)
        return 0

    lax.fori_loop(0, n_chunks + LAGS[-1], iteration, 0)

    def drain(t, _):
        for copy in (pair_sum(t),) + scatter1(t) + scatter2(t) + gather1(t) + gather2(t) + pair_copy(t):
            copy.wait_send()
        return 0

    lax.fori_loop(0, n_chunks, drain, 0)


ANY = pl.BlockSpec(memory_space=pl.ANY)
VM = pl.BlockSpec(memory_space=pltpu.VMEM)
SM = pl.BlockSpec(memory_space=pltpu.SMEM)
LIMIT = 62 << 20


def solution(mesh):
    def local_step(tokens, lengths, k_cache, v_cache, norm_gain, w_query, w_key, w_value, w_out, w_gate, w_up, w_down):
        batch, width = tokens.shape
        rows = batch // PEERS
        heads = width // 128
        n_chunks = width // BLOCK
        dma = pltpu.SemaphoreType.DMA

        q_all, key_new, value_new, normed, early = pl.pallas_call(
            project_kernel,
            name="project",
            out_shape=(
                jax.ShapeDtypeStruct((heads, rows, 128), BF16),
                jax.ShapeDtypeStruct((rows, 128), BF16),
                jax.ShapeDtypeStruct((rows, 128), BF16),
                jax.ShapeDtypeStruct((batch, width), BF16),
                jax.ShapeDtypeStruct((batch, EARLY * BLOCK // 2), BF16),
            ),
            in_specs=[ANY, VM, VM, ANY, ANY, ANY, ANY, ANY],
            out_specs=(VM, VM, VM, ANY, VM),
            scratch_shapes=[
                pltpu.VMEM((batch, width), BF16),
                pltpu.VMEM((batch, width), BF16),
                pltpu.VMEM((SLOTS, width, BLOCK), BF16),
                pltpu.VMEM((6, batch, 128), BF16),
                pltpu.VMEM((batch, 128), F32),
                pltpu.VMEM((batch, 128), F32),
                dma, dma((SLOTS, 3)), dma, dma((PEERS,)), dma((PEERS,)),
            ],
            compiler_params=pltpu.CompilerParams(collective_id=0, has_side_effects=True, vmem_limit_bytes=LIMIT),
        )(tokens, lengths.reshape(batch, 1), norm_gain.reshape(1, width), w_query, w_key, w_value, w_gate, w_up)

        attended = pl.pallas_call(
            attend_kernel,
            name="attend",
            out_shape=jax.ShapeDtypeStruct((heads, rows, 128), BF16),
            in_specs=[SM, VM, VM, VM, ANY, ANY],
            out_specs=VM,
            scratch_shapes=[
                pltpu.VMEM((rows, heads, 128), F32),
                pltpu.VMEM((rows, heads, 128), F32),
                pltpu.VMEM((rows, 128), F32),
                pltpu.VMEM((rows, 128), F32),
                pltpu.VMEM((RING * ITEMS, CHUNK, 128), BF16),
                pltpu.VMEM((RING * ITEMS, CHUNK, 128), BF16),
                pltpu.SMEM((rows * (4096 // CHUNK) + ITEMS,), jnp.int32),
                pltpu.SMEM((rows * (4096 // CHUNK) + ITEMS,), jnp.int32),
                pltpu.VMEM((heads, 1), F32),
                pltpu.VMEM((heads, 1), F32),
                pltpu.VMEM((heads, 128), F32),
                dma((RING * ITEMS,)), dma((RING * ITEMS,)),
            ],
            compiler_params=pltpu.CompilerParams(vmem_limit_bytes=LIMIT),
        )(lengths, q_all, key_new, value_new, k_cache, v_cache)

        y = pl.pallas_call(
            combine_kernel,
            name="combine",
            out_shape=jax.ShapeDtypeStruct((batch, width), BF16),
            in_specs=[VM, ANY, ANY, ANY, ANY, ANY, ANY, ANY],
            out_specs=VM,
            scratch_shapes=[
                pltpu.VMEM((batch, width), BF16),
                pltpu.VMEM((batch, w_out.shape[0] + w_down.shape[0]), BF16),
                pltpu.VMEM((SLOTS, width, BLOCK), BF16),
                pltpu.VMEM((6, batch, 128), BF16),
                pltpu.VMEM((2, 16, width), BF16),
                pltpu.VMEM((n_chunks, batch, BLOCK), F32),
                pltpu.VMEM((n_chunks, 128, BLOCK), F32),
                pltpu.VMEM((n_chunks, 32, BLOCK), F32),
                pltpu.VMEM((n_chunks, 32, BLOCK), F32),
                pltpu.VMEM((n_chunks, 16, BLOCK), F32),
                pltpu.VMEM((n_chunks, 16, BLOCK), F32),
                dma, dma, dma((2,)), dma((SLOTS, 2)), dma((PEERS,)), dma((PEERS,)),
                dma((10, n_chunks)), dma((10, n_chunks)),
            ],
            compiler_params=pltpu.CompilerParams(collective_id=1, has_side_effects=True, vmem_limit_bytes=LIMIT),
        )(attended, tokens, normed, early, w_gate, w_up, w_out, w_down)
        return y, key_new.reshape(rows, 1, 128), value_new.reshape(rows, 1, 128)

    in_specs = (P('replica', None), P('replica'), P('replica', None, None, None), P('replica', None, None, None), P(None), P(None, 'model'), P(None, None), P(None, None), P('model', None), P(None, 'model'), P(None, 'model'), P('model', None))
    out_specs = (P('replica', None), P(('replica', 'model'), None, None), P(('replica', 'model'), None, None))
    return jax.shard_map(local_step, mesh=mesh, in_specs=in_specs, out_specs=out_specs, check_vma=False)
```

time: 264 us -> 127 us (0.48)
  matrix products: 120 us -> 0 us
  Pallas kernels: 0 us -> 120 us
  waiting for transfers between devices: 93 us -> 0 us
  other arithmetic: 26.5 us -> 0 us
  between operations: 14.2 us -> 0.67 us
  starting transfers between devices: 7.49 us -> 0 us
  local copies, waits for them, and re-layouts: 2.21 us -> 7.89 us
    dot_general x10 -> x0, matrix products: 120 us -> none  [the longest x1 23.2 us: attend(): jnp.einsum('bgrd,bgtd->bgrt', grouped, key_rows, preferred_element_type=j...]
    pallas_call x0 -> x3, Pallas kernels: none -> 120 us  [the longest x1 77.4 us: local_step(): pl.pallas_call(combine_kernel, name='combine', out_shape=jax.ShapeDtypeSt...]
    psum x1 -> x0, waiting for transfers between devices: 93 us -> none  [local_step(): summed = lax.psum(partial_sum, 'model')]
    reduce_sum x2 -> x0, other arithmetic: 14.3 us -> none  [the longest x1 11.5 us: attend(): total = jnp.sum(weights, axis=-1) + weight_new]
    convert_element_type x6 -> x0, other arithmetic: 10.7 us -> none  [the longest x1 6.21 us: local_step(): (tokens.astype(jnp.float32) + summed).astype(jnp.bfloat16)]
    all_to_all x2 -> x0, starting transfers between devices: 7.23 us -> none  [the longest x1 4.3 us: local_step(): queries = lax.all_to_all(queries, 'model', 0, 1, tiled=True)]
    unnamed x10 -> x7, local copies, waits for them, and re-layouts: 0.03 us -> 5.09 us
    reshape x0 -> x2, local copies, waits for them, and re-layouts: none -> 2.8 us  [the longest x1 1.47 us: local_step(): lengths.reshape(batch, 1)]
  transfers between devices with their start and end apart: 3 -> 0, of which waited for: 1 -> 0; matrix products, arithmetic and copies ran while one was open for 16% -> 0% of each run, Pallas kernels for 0% -> 0%
where the time goes in v1:
time: 127 us; the launch traced here: 128 us
  Pallas kernels  120 us (94%)
  local copies, waits for them, and re-layouts  7.89 us (6%)
    pallas_call x1, Pallas kernels, local_step(): pl.pallas_call(combine_kernel, name='combine', out_shape=jax.ShapeDtypeSt...  77.4 us
    pallas_call x1, Pallas kernels, local_step(): pl.pallas_call(project_kernel, name='project', out_shape=(jax.ShapeDtypeS...  24.4 us
    pallas_call x1, Pallas kernels, local_step(): pl.pallas_call(attend_kernel, name='attend', out_shape=jax.ShapeDtypeStru...  17.9 us
    unnamed x7, local copies, waits for them, and re-layouts  5.09 us

profile of v1, /device:TPU:0, one launch (start us, length us, event | category | flops | bytes accessed | tf_op | source)
XLA Modules:
  0.0 128.2 jit_solution(15019190220394030287)
XLA Ops:
  0.6 1.3 %reshape.19.gain_ref = bf16[1,6144]{1,0:T(2,128)(2,1)} reshape(bf16[6144]{0:T(1024)(128)(2,1)} %param.16) | data formatting | bytes 24576 | tf_op jit(solution)/shard_map/reshape | solution.py:472
  2.0 1.5 %copy.15.lengths_ref = s32[256,1]{1,0:T(8,128)} copy(s32[256,1]{0,1:T(1,128)} %bitcast.5) | data formatting | bytes 2048 | tf_op jit(solution)/shard_map/reshape | solution.py:472
  3.4 24.4 %project.1 = (bf16[48,32,128]{2,1,0:T(8,128)(2,1)}, bf16[32,128]{1,0:T(8,128)(2,1)}, bf16[32,128]{1,0:T(8,128)(2,1)}, bf16[256,6144]{1,0:T(8,128)(2,1)}, bf16[256,1280]{1,0:T(8,128)(2,1)}) custom-call(bf16[256,6144]{1,0:T(8,128)(2,1)} %x_hbm.3, s32[256,1]{1,0:T(8,128)} %copy.15.lengths_ref, bf16[1,6144]{1,0:T(2,128)(2,1)} %reshape.19.gain_ref, ...), custom_call_target="tpu_custom_call" | custom-call | tf_op jit(solution)/shard_map/project/pallas_call | solution.py:450
  27.9 17.9 %attend.1.o_ref = bf16[48,32,128]{2,1,0:T(8,128)(2,1)} custom-call(s32[256]{0:T(256)} %lengths_ref.1, bf16[48,32,128]{2,1,0:T(8,128)(2,1)} %get-tuple-element.8.q_ref, bf16[32,128]{1,0:T(8,128)(2,1)} %get-tuple-element.9.knew_ref, bf16[32,128]{1,0:T(8,128)(2,1)} %get-tuple-element.10.vnew_ref, bf16[256,1,4096,128]{3,2,1,0:T(8,128)(2,1)} %k_hbm.1, ...), custom_call_target="tpu_custom_call" | custom-call | tf_op jit(solution)/shard_map/attend/pallas_call | solution.py:474
  45.7 0.0 copy-start.1
  45.7 0.0 copy-start
  45.8 77.4 %combine.1 = bf16[256,6144]{1,0:T(8,128)(2,1)} custom-call(bf16[48,32,128]{2,1,0:T(8,128)(2,1)} %attend.1.o_ref, bf16[256,6144]{1,0:T(8,128)(2,1)} %x_hbm.3, bf16[256,6144]{1,0:T(8,128)(2,1)} %get-tuple-element.11.normed_hbm, bf16[256,1280]{1,0:T(8,128)(2,1)} %get-tuple-element.12.early_hbm, bf16[6144,3072]{1,0:T(8,128)(2,1)} %gate_hbm.3, ...), custom_call_target="tpu_custom_call" | custom-call | tf_op jit(solution)/shard_map/combine/pallas_call | solution.py:497
  123.2 3.9 %copy.19 = bf16[256,6144]{1,0:T(8,128)(2,1)} copy(bf16[256,6144]{1,0:T(8,128)(2,1)} %combine.1) | data formatting | bytes 6291456
  127.0 0.0 copy-done.1
  127.0 0.6 copy.20
  127.6 0.0 copy-done
  127.6 0.6 copy.21
Async XLA Ops:
  45.7 81.3 %copy-start.1 = (bf16[32,128]{1,0:T(8,128)(2,1)S(1)}, bf16[32,128]{1,0:T(8,128)(2,1)}, u32[]{:S(2)}) copy-start(bf16[32,128]{1,0:T(8,128)(2,1)} %get-tuple-element.9.knew_ref) | copy-start | bytes 24580
  45.7 81.9 %copy-start = (bf16[32,128]{1,0:T(8,128)(2,1)S(1)}, bf16[32,128]{1,0:T(8,128)(2,1)}, u32[]{:S(2)}) copy-start(bf16[32,128]{1,0:T(8,128)(2,1)} %get-tuple-element.10.vnew_ref) | copy-start | bytes 24580

commit v2 on v1

v2 whole, which is shorter than its diff:
```python
import functools
import math
import jax
import jax.numpy as jnp
from jax import lax
from jax.experimental import pallas as pl
from jax.experimental.pallas import tpu as pltpu
from jax.sharding import PartitionSpec as P

ROPE_BASE = 10000.0
NORM_EPS = 1e-6
MASK_VALUE = -1e30
BF16, F32 = jnp.bfloat16, jnp.float32
MESH = pl.DeviceIdType.MESH

PEERS = 8
SLOTS = 4
BLOCK = 512
EARLY = 4
CHUNK = 512
ITEMS = 4
RING = 3
CHUNK_COLS = 512
LAGS = (0, 1, 4, 10, 14, 18, 19)


def greet(me):
    barrier = pltpu.get_barrier_semaphore()
    for step in range(1, PEERS):
        peer = lax.rem(me + step, PEERS)
        pl.semaphore_signal(barrier, inc=1, device_id={"model": peer}, device_id_type=MESH)
    return barrier


def gate_up_copies(block, slot, gate_hbm, up_hbm, ring, sems):
    half = BLOCK // 2
    columns = pl.ds(pl.multiple_of(block * half, half), half)
    return (
        pltpu.make_async_copy(gate_hbm.at[:, columns], ring.at[slot, :, pl.ds(0, half)], sems.at[slot, 0]),
        pltpu.make_async_copy(up_hbm.at[:, columns], ring.at[slot, :, pl.ds(half, half)], sems.at[slot, 1]),
    )


def hidden_block(normed, weights):
    half = BLOCK // 2
    both = jnp.dot(normed, weights, preferred_element_type=F32)
    gate, up = both[:, :half], both[:, half:]
    return (gate * lax.logistic(gate) * up).astype(BF16)


def rope(values, cos_part, sin_part):
    return values * cos_part + pltpu.roll(values, 64, 1) * sin_part


def project_kernel(x_hbm, lengths_hbm, gain_hbm, wq_hbm, wk_hbm, wv_hbm, gate_hbm, up_hbm,
                   q_out, knew_ref, vnew_ref, normed, hidden_ref,
                   x_ref, lengths_ref, gain_ref, ring, q_scr, cos_scr, sin_scr, stat_scr, gain_scr, x_sem, in_sem, sems, send_sem, recv_sem):
    me = lax.axis_index("model")
    batch = x_ref.shape[0]
    width = x_ref.shape[1]
    rows = batch // PEERS
    barrier = greet(me)
    x_copy = pltpu.make_async_copy(x_hbm, x_ref, x_sem)
    l_copy = pltpu.make_async_copy(lengths_hbm, lengths_ref, in_sem.at[0])
    g_copy = pltpu.make_async_copy(gain_hbm, gain_ref, in_sem.at[1])
    for copy in (l_copy, x_copy, g_copy):
        copy.start()
    first = (pltpu.make_async_copy(wq_hbm.at[:, pl.ds(0, 512)], ring.at[0], sems.at[0, 0]),)
    second = (
        pltpu.make_async_copy(wq_hbm.at[:, pl.ds(512, 256)], ring.at[1, :, pl.ds(0, 256)], sems.at[1, 0]),
        pltpu.make_async_copy(wk_hbm, ring.at[1, :, pl.ds(256, 128)], sems.at[1, 1]),
        pltpu.make_async_copy(wv_hbm, ring.at[1, :, pl.ds(384, 128)], sems.at[1, 2]),
    )
    gu = lambda block, slot: gate_up_copies(block, slot, gate_hbm, up_hbm, ring, sems)

    hb = batch // 2
    l_copy.wait()
    spread = jnp.broadcast_to(lengths_ref[...].astype(F32).reshape(1, batch), (128, batch)).T
    lane = lax.broadcasted_iota(jnp.int32, (hb, 128), 1)
    low = lane < 64
    pair = jnp.where(low, lane, lane - 64).astype(F32)
    inv_freq = jnp.exp(pair * (-2.0 * math.log(ROPE_BASE) / 128))
    angles = jnp.where(low, spread[:hb], spread[hb:]) * inv_freq
    cos_part, sin_part = jnp.cos(angles), jnp.sin(angles)
    cos_turn, sin_turn = pltpu.roll(cos_part, 64, 1), pltpu.roll(sin_part, 64, 1)
    cos_scr[:hb] = jnp.where(low, cos_part, cos_turn)
    cos_scr[hb:] = jnp.where(low, cos_turn, cos_part)
    sin_scr[:hb] = jnp.where(low, -sin_part, sin_turn)
    sin_scr[hb:] = jnp.where(low, -sin_turn, sin_part)

    x_copy.wait()
    for copy in first:
        copy.start()
    tiles = width // 128

    def square_rows(r, _):
        at = pl.ds(pl.multiple_of(r * 16, 16), 16)
        sums = [jnp.zeros((16, 128), F32) for _ in range(4)]
        for j in range(tiles):
            values = x_ref[at, j * 128:(j + 1) * 128].astype(F32)
            sums[j % 4] = sums[j % 4] + values * values
        stat_scr[at, :] = (sums[0] + sums[1]) + (sums[2] + sums[3])
        return 0

    lax.fori_loop(0, batch // 16, square_rows, 0)
    mean_sq = jnp.sum(stat_scr[...], axis=-1, keepdims=True) * (1.0 / width)
    stat_scr[...] = jnp.broadcast_to(lax.rsqrt(mean_sq + NORM_EPS), (batch, 128))

    def norm_rows(r, _):
        at = pl.ds(pl.multiple_of(r * 16, 16), 16)
        factor = stat_scr[at, :]
        for j in range(tiles):
            cols = slice(j * 128, (j + 1) * 128)
            normed[at, cols] = (x_ref[at, cols].astype(F32) * factor * gain_scr[:, cols]).astype(BF16)
        return 0

    for copy in second:
        copy.start()
    g_copy.wait()
    gain_scr[...] = gain_ref[...].astype(F32).reshape(1, width)
    lax.fori_loop(0, batch // 16, norm_rows, 0)

    for copy in first:
        copy.wait()
    for copy in gu(0, 2):
        copy.start()
    head4 = jnp.dot(normed[...], ring[0], preferred_element_type=F32)
    for h in range(4):
        q_scr[h] = rope(head4[:, h * 128:(h + 1) * 128], cos_scr[...], sin_scr[...]).astype(BF16)
    for copy in second:
        copy.wait()
    for copy in gu(1, 3) + gu(2, 0):
        copy.start()
    tail = jnp.dot(normed[...], ring[1], preferred_element_type=F32)
    for h in range(2):
        q_scr[4 + h] = rope(tail[:, h * 128:(h + 1) * 128], cos_scr[...], sin_scr[...]).astype(BF16)
    k_all = rope(tail[:, 256:384], cos_scr[...], sin_scr[...])
    cos_scr[...] = k_all
    sin_scr[...] = tail[:, 384:512]
    mine = pl.ds(pl.multiple_of(me * rows, rows), rows)
    knew_ref[...] = cos_scr[mine, :].astype(BF16)
    vnew_ref[...] = sin_scr[mine, :].astype(BF16)
    for copy in gu(3, 1):
        copy.start()

    pl.semaphore_wait(barrier, PEERS - 1)
    heads = pl.ds(me * 6, 6)
    sends = []
    for step in range(1, PEERS):
        peer = lax.rem(me + step, PEERS)
        sends.append(pltpu.make_async_remote_copy(
            src_ref=q_scr.at[:, pl.ds(pl.multiple_of(peer * rows, rows), rows), :],
            dst_ref=q_out.at[heads],
            send_sem=send_sem.at[step], recv_sem=recv_sem.at[step],
            device_id={"model": peer}, device_id_type=MESH))
        sends[-1].start()
    q_out[heads] = q_scr[:, mine, :]

    half = BLOCK // 2

    def block_step(n, _):
        slot = lax.rem(n + 2, SLOTS)
        for copy in gu(n, slot):
            copy.wait()
        hidden_ref[:, pl.ds(pl.multiple_of(n * half, half), half)] = hidden_block(normed[...], ring[slot])

        @pl.when(n + SLOTS < EARLY)
        def _():
            for copy in gu(n + SLOTS, slot):
                copy.start()
        return 0

    lax.fori_loop(0, EARLY, block_step, 0)
    for copy in sends:
        copy.wait()


def attend_kernel(lengths_ref, q_in, k16, v16, k_hbm, v_hbm, o_ref, key_out, value_out,
                  q_scr, o_scr, k_scr, v_scr, k_buf, v_buf, item_row, item_chunk, m_run, l_run, acc_run,
                  k_sem, v_sem, out_sem):
    me = lax.axis_index("model")
    rows = o_ref.shape[1]
    head_count = o_ref.shape[0]
    context = k_hbm.shape[2]
    base = me * rows
    scale = 128 ** -0.5
    def chunks_of(b):
        return lax.div(lengths_ref[base + b] + (CHUNK - 1), CHUNK)

    total = chunks_of(0)
    for b in range(1, rows):
        total = total + chunks_of(b)
    bodies = lax.div(total + (ITEMS - 1), ITEMS)

    def copies(g, j):
        n = g * ITEMS + j
        start = pl.multiple_of(jnp.minimum(item_chunk[n] * CHUNK, context - CHUNK), CHUNK)
        row = base + item_row[n]
        slot = lax.rem(g, RING) * (ITEMS // 2) + j // 2
        sem = lax.rem(g, RING) * ITEMS + j
        src, lanes = pl.ds(start, CHUNK), pl.ds(128 * (j % 2), 128)
        return (pltpu.make_async_copy(k_hbm.at[row, 0, src, :], k_buf.at[slot, :, lanes], k_sem.at[sem]),
                pltpu.make_async_copy(v_hbm.at[row, 0, src, :], v_buf.at[slot, :, lanes], v_sem.at[sem]))

    def launch(g, state):
        b, c = state
        for j in range(ITEMS):
            n = g * ITEMS + j
            item_row[n] = b
            item_chunk[n] = c
            turn = (c + 1 >= chunks_of(b)) & (b < rows - 1)
            b, c = jnp.where(turn, b + 1, b), jnp.where(turn, 0, c + 1)

        @pl.when(g < bodies)
        def _():
            for j in range(ITEMS):
                for copy in copies(g, j):
                    copy.start()
        return b, c

    state = (jnp.int32(0), jnp.int32(0))
    for g in range(RING - 1):
        state = launch(g, state)

    outputs = [pltpu.make_async_copy(k16, key_out, out_sem.at[0]), pltpu.make_async_copy(v16, value_out, out_sem.at[1])]
    for copy in outputs:
        copy.start()
    k_scr[...] = k16[...].astype(F32)
    v_scr[...] = v16[...].astype(F32)
    q_scr[...] = jnp.swapaxes(q_in[...].astype(F32), 0, 1).astype(BF16)
    m_run[...] = jnp.zeros_like(m_run)
    l_run[...] = jnp.ones_like(l_run)
    acc_run[...] = jnp.zeros_like(acc_run)

    def body(g, state):
        state = launch(g + RING - 1, state)
        for j in range(ITEMS):
            for copy in copies(g, j):
                copy.wait()
        m, l, acc = m_run[...], l_run[...], acc_run[...]
        blank = jnp.zeros((head_count, 128), BF16)
        scored = []
        for p in range(ITEMS // 2):
            slot = lax.rem(g, RING) * (ITEMS // 2) + p
            news, q_rows = [], []
            for j in range(2):
                n = g * ITEMS + 2 * p + j
                b, c = item_row[n], item_chunk[n]
                q16 = q_scr[b]
                q32 = q16.astype(F32)
                q_rows.append(jnp.concatenate([q16, blank] if j == 0 else [blank, q16], axis=1))
                s_new = jnp.sum(q32 * k_scr[pl.ds(b, 1), :], axis=-1, keepdims=True) * scale
                news.append((b, c, s_new, lengths_ref[base + b] - c * CHUNK))
            s_pair = lax.dot_general(jnp.concatenate(q_rows, axis=0), k_buf[slot], (((1,), (1,)), ((), ())), preferred_element_type=F32) * scale
            for j in range(2):
                b, c, s_new, left = news[j]
                s = s_pair[j * head_count:(j + 1) * head_count]
                s = jnp.where(lax.broadcasted_iota(jnp.int32, s.shape, 1) < left, s, MASK_VALUE)
                scored.append((s, jnp.max(s, axis=-1, keepdims=True), s_new, b, c))
        for p in range(ITEMS // 2):
            slot = lax.rem(g, RING) * (ITEMS // 2) + p
            tops, weights, shrinks = [], [], []
            for j in range(2):
                s, s_max, s_new, b, c = scored[2 * p + j]
                m_prev = jnp.where(c == 0, s_new, m)
                m = jnp.maximum(m_prev, s_max)
                e = jnp.exp(s - m)
                shrink = jnp.exp(m_prev - m)
                l = jnp.where(c == 0, 1.0, l) * shrink + jnp.sum(e, axis=-1, keepdims=True)
                tops.append(l)
                shrinks.append(shrink)
                weights.append(e.astype(BF16))
            mixed = jnp.dot(jnp.concatenate(weights, axis=0), v_buf[slot], preferred_element_type=F32)
            for j in range(2):
                _, _, _, b, c = scored[2 * p + j]
                part = mixed[j * head_count:(j + 1) * head_count, j * 128:(j + 1) * 128]
                acc = jnp.where(c == 0, v_scr[pl.ds(b, 1), :], acc) * shrinks[j] + part
                o_scr[b] = acc / tops[j]
        m_run[...], l_run[...], acc_run[...] = m, l, acc
        return state

    lax.fori_loop(0, bodies, body, state)
    for copy in outputs:
        copy.wait()
    o_ref[...] = jnp.swapaxes(o_scr[...], 0, 1).astype(BF16)


def combine_kernel(o_ref, x_hbm, normed, early_ref, gate_hbm, up_hbm, wo_hbm, wd_hbm, y_ref,
                   act, ring, o_full, x_rows, part, pair_in, in1x, in1y, in2x, in2y,
                   x_sem, sems, o_send, o_recv, c_send, c_recv):
    me = lax.axis_index("model")
    core = lax.rem(me, 2)
    xi = lax.rem(lax.div(me, 2), 2)
    yi = lax.div(me, 4)
    partner = me + 1 - 2 * core
    x_peer = me + 2 - 4 * xi
    y_peer = me + 4 - 8 * yi
    batch = normed.shape[0]
    rows = batch // PEERS
    late = gate_hbm.shape[1] // (BLOCK // 2) - EARLY
    n_chunks = y_ref.shape[1] // CHUNK_COLS
    o_width = wo_hbm.shape[0]
    f_width = wd_hbm.shape[0]
    half = BLOCK // 2
    barrier = greet(me)

    early_width = EARLY * half

    def gu(n, slot):
        return gate_up_copies(n + EARLY, slot, gate_hbm, up_hbm, ring, sems)

    def down(t, slot):
        columns = pl.ds(pl.multiple_of(t * CHUNK_COLS, CHUNK_COLS), CHUNK_COLS)
        lanes = pl.ds(0, CHUNK_COLS)
        return (
            pltpu.make_async_copy(wo_hbm.at[:, columns], ring.at[slot, pl.ds(0, o_width), lanes], sems.at[slot, 0]),
            pltpu.make_async_copy(wd_hbm.at[:, columns], ring.at[slot, pl.ds(o_width, f_width), lanes], sems.at[slot, 1]),
        )

    def fetch(n):
        slot = lax.rem(n, SLOTS)

        @pl.when(n < late)
        def _():
            for copy in gu(n, slot):
                copy.start()

        @pl.when((n >= late) & (n < late + n_chunks))
        def _():
            for copy in down(n - late, slot):
                copy.start()

    for copy in gu(0, 0):
        copy.start()
    row_x = core * 128 + xi * 32 + yi * 16
    row_y = core * 128 + 64 + yi * 32 + xi * 16
    x_copies = []
    for k, row in enumerate((row_x, row_y)):
        x_copies.append(pltpu.make_async_copy(x_hbm.at[pl.ds(pl.multiple_of(row, 16), 16), :], x_rows.at[k], x_sem.at[k]))
    pl.semaphore_wait(barrier, PEERS - 1)
    mine = pl.ds(pl.multiple_of(me * rows, rows), rows)
    sends = []
    for step in range(1, PEERS):
        peer = lax.rem(me + step, PEERS)
        sends.append(pltpu.make_async_remote_copy(
            src_ref=o_ref.at[pl.ds(peer * 6, 6)], dst_ref=o_full.at[:, mine, :],
            send_sem=o_send.at[step], recv_sem=o_recv.at[step],
            device_id={"model": peer}, device_id_type=MESH))
        sends[-1].start()
    o_full[:, mine, :] = o_ref[pl.ds(me * 6, 6)]
    act[:, o_width:o_width + early_width] = early_ref[...]
    for copy in gu(1, 1):
        copy.start()

    def block_step(n, _):
        slot = lax.rem(n, SLOTS)
        for copy in gu(n, slot):
            copy.wait()

        @pl.when(n == 0)
        def _():
            fetch(2)
            fetch(3)
        at = pl.ds(pl.multiple_of(o_width + early_width + n * half, half), half)
        act[:, at] = hidden_block(normed[...], ring[slot])
        fetch(n + SLOTS)
        return 0

    lax.fori_loop(0, late - 1, block_step, 0)
    for copy in x_copies:
        copy.start()
    block_step(late - 1, 0)
    for copy in x_copies:
        copy.wait()
    for copy in sends:
        copy.wait()
    for h in range(6):
        act[:, h * 128:(h + 1) * 128] = o_full[h]

    my_half = pl.multiple_of(core * 128, 128)
    other_half = pl.multiple_of(128 - core * 128, 128)
    keep1x = pl.multiple_of(my_half + xi * 32, 32)
    give1x = pl.multiple_of(my_half + 32 - xi * 32, 32)
    keep1y = pl.multiple_of(my_half + 64 + yi * 32, 32)
    give1y = pl.multiple_of(my_half + 96 - yi * 32, 32)
    keep2x = pl.multiple_of(keep1x + yi * 16, 16)
    give2x = pl.multiple_of(keep1x + 16 - yi * 16, 16)
    keep2y = pl.multiple_of(keep1y + xi * 16, 16)
    give2y = pl.multiple_of(keep1y + 16 - xi * 16, 16)

    def cols(t):
        return pl.ds(pl.multiple_of(t * CHUNK_COLS, CHUNK_COLS), CHUNK_COLS)

    def remote(kind, t, src, dst, peer):
        return pltpu.make_async_remote_copy(
            src_ref=src, dst_ref=dst, send_sem=c_send.at[kind, t], recv_sem=c_recv.at[kind, t],
            device_id={"model": peer}, device_id_type=MESH)

    def pair_sum(t):
        return remote(0, t, part.at[t, pl.ds(other_half, 128), :], pair_in.at[t], partner)

    def scatter1(t):
        return (remote(1, t, part.at[t, pl.ds(give1x, 32), :], in1x.at[t], x_peer),
                remote(2, t, part.at[t, pl.ds(give1y, 32), :], in1y.at[t], y_peer))

    def scatter2(t):
        return (remote(3, t, part.at[t, pl.ds(give2x, 16), :], in2x.at[t], y_peer),
                remote(4, t, part.at[t, pl.ds(give2y, 16), :], in2y.at[t], x_peer))

    def spread(kind, t, row, count, peer):
        at = y_ref.at[pl.ds(row, count), cols(t)]
        return remote(kind, t, at, at, peer)

    def gather1(t):
        return spread(5, t, keep2x, 16, y_peer), spread(6, t, keep2y, 16, x_peer)

    def gather2(t):
        return spread(7, t, keep1x, 32, x_peer), spread(8, t, keep1y, 32, y_peer)

    def pair_copy(t):
        return (spread(9, t, my_half, 128, partner),)

    def start(copies):
        for copy in copies:
            copy.start()

    def arrive(copies):
        for copy in copies:
            copy.wait_recv()

    def stage_compute(t):
        slot = lax.rem(t + late, SLOTS)
        for copy in down(t, slot):
            copy.wait()
        part[t] = jnp.dot(act[...], ring[slot, pl.ds(0, o_width + f_width), pl.ds(0, CHUNK_COLS)], preferred_element_type=F32)
        pair_sum(t).start()
        fetch(t + late + SLOTS)

    def stage_scatter1(t):
        pair_sum(t).wait_recv()
        part[t, pl.ds(my_half, 128), :] = part[t, pl.ds(my_half, 128), :] + pair_in[t]
        start(scatter1(t))

    def stage_scatter2(t):
        arrive(scatter1(t))
        part[t, pl.ds(keep1x, 32), :] = part[t, pl.ds(keep1x, 32), :] + in1x[t]
        part[t, pl.ds(keep1y, 32), :] = part[t, pl.ds(keep1y, 32), :] + in1y[t]
        start(scatter2(t))

    def stage_gather1(t):
        arrive(scatter2(t))
        for k, (keep, inbox) in enumerate(((keep2x, in2x), (keep2y, in2y))):
            total = part[t, pl.ds(keep, 16), :] + inbox[t]
            y_ref[pl.ds(keep, 16), cols(t)] = (x_rows[k, :, cols(t)].astype(F32) + total).astype(BF16)
        start(gather1(t))

    def stage_gather2(t):
        arrive(gather1(t))
        start(gather2(t))

    def stage_pair(t):
        arrive(gather2(t))
        start(pair_copy(t))

    def stage_end(t):
        arrive(pair_copy(t))

    stages = (stage_compute, stage_scatter1, stage_scatter2, stage_gather1, stage_gather2, stage_pair, stage_end)

    def iteration(i, _):
        for lag, stage in zip(LAGS, stages):
            t = i - lag

            @pl.when((t >= 0) & (t < n_chunks))
            def _(stage=stage, t=t):
                stage(t)
        return 0

    lax.fori_loop(0, n_chunks + LAGS[-1], iteration, 0)

    def drain(t, _):
        for copy in (pair_sum(t),) + scatter1(t) + scatter2(t) + gather1(t) + gather2(t) + pair_copy(t):
            copy.wait_send()
        return 0

    lax.fori_loop(0, n_chunks, drain, 0)


ANY = pl.BlockSpec(memory_space=pltpu.HBM)
VM = pl.BlockSpec(memory_space=pltpu.VMEM)
SM = pl.BlockSpec(memory_space=pltpu.SMEM)
LIMIT = 50 << 20


def project_call(tokens, lengths, norm_gain, w_query, w_key, w_value, w_gate, w_up):
    lengths, norm_gain = (pltpu.with_memory_space_constraint(a, pltpu.HBM) for a in (lengths, norm_gain))
    batch, width = tokens.shape
    rows = batch // PEERS
    dma = pltpu.SemaphoreType.DMA
    return pl.pallas_call(
        project_kernel,
        name="project",
        out_shape=(
            pltpu.VMEM((width // 128, rows, 128), BF16),
            pltpu.VMEM((rows, 128), BF16),
            pltpu.VMEM((rows, 128), BF16),
            pltpu.VMEM((batch, width), BF16),
            pltpu.VMEM((batch, EARLY * BLOCK // 2), BF16),
        ),
        in_specs=[ANY, ANY, ANY, ANY, ANY, ANY, ANY, ANY],
        out_specs=(VM, VM, VM, VM, VM),
        scratch_shapes=[
            pltpu.VMEM((batch, width), BF16),
            pltpu.VMEM((batch,), jnp.int32),
            pltpu.VMEM((width,), BF16),
            pltpu.VMEM((SLOTS, width, BLOCK), BF16),
            pltpu.VMEM((6, batch, 128), BF16),
            pltpu.VMEM((batch, 128), F32),
            pltpu.VMEM((batch, 128), F32),
            pltpu.VMEM((batch, 128), F32),
            pltpu.VMEM((1, width), F32),
            dma, dma((2,)), dma((SLOTS, 3)), dma((PEERS,)), dma((PEERS,)),
        ],
        compiler_params=pltpu.CompilerParams(collective_id=0, has_side_effects=True, vmem_limit_bytes=LIMIT),
    )(tokens, lengths, norm_gain, w_query, w_key, w_value, w_gate, w_up)


def attend_call(lengths, q_all, key_new, value_new, k_cache, v_cache):
    heads, rows, _ = q_all.shape
    dma = pltpu.SemaphoreType.DMA
    return pl.pallas_call(
        attend_kernel,
        name="attend",
        out_shape=(
            pltpu.VMEM((heads, rows, 128), BF16),
            jax.ShapeDtypeStruct((rows, 128), BF16),
            jax.ShapeDtypeStruct((rows, 128), BF16),
        ),
        in_specs=[SM, VM, VM, VM, ANY, ANY],
        out_specs=(VM, ANY, ANY),
        scratch_shapes=[
            pltpu.VMEM((rows, heads, 128), BF16),
            pltpu.VMEM((rows, heads, 128), F32),
            pltpu.VMEM((rows, 128), F32),
            pltpu.VMEM((rows, 128), F32),
            pltpu.VMEM((RING * ITEMS // 2, CHUNK, 256), BF16),
            pltpu.VMEM((RING * ITEMS // 2, CHUNK, 256), BF16),
            pltpu.SMEM((rows * (k_cache.shape[2] // CHUNK) + RING * ITEMS,), jnp.int32),
            pltpu.SMEM((rows * (k_cache.shape[2] // CHUNK) + RING * ITEMS,), jnp.int32),
            pltpu.VMEM((heads, 1), F32),
            pltpu.VMEM((heads, 1), F32),
            pltpu.VMEM((heads, 128), F32),
            dma((RING * ITEMS,)), dma((RING * ITEMS,)), dma((2,)),
        ],
        compiler_params=pltpu.CompilerParams(vmem_limit_bytes=20 << 20),
    )(lengths, q_all, key_new, value_new, k_cache, v_cache)


def combine_call(attended, tokens, normed, early, w_gate, w_up, w_out, w_down):
    attended, normed, early = (pltpu.with_memory_space_constraint(a, pltpu.VMEM) for a in (attended, normed, early))
    batch, width = tokens.shape
    n_chunks = width // CHUNK_COLS
    dma = pltpu.SemaphoreType.DMA
    return pl.pallas_call(
        combine_kernel,
        name="combine",
        out_shape=pltpu.VMEM((batch, width), BF16),
        in_specs=[VM, ANY, VM, VM, ANY, ANY, ANY, ANY],
        out_specs=VM,
        scratch_shapes=[
            pltpu.VMEM((batch, w_out.shape[0] + w_down.shape[0]), BF16),
            pltpu.VMEM((SLOTS, width, BLOCK), BF16),
            pltpu.VMEM((6, batch, 128), BF16),
            pltpu.VMEM((2, 16, width), BF16),
            pltpu.VMEM((n_chunks, batch, CHUNK_COLS), F32),
            pltpu.VMEM((n_chunks, 128, CHUNK_COLS), F32),
            pltpu.VMEM((n_chunks, 32, CHUNK_COLS), F32),
            pltpu.VMEM((n_chunks, 32, CHUNK_COLS), F32),
            pltpu.VMEM((n_chunks, 16, CHUNK_COLS), F32),
            pltpu.VMEM((n_chunks, 16, CHUNK_COLS), F32),
            dma((2,)), dma((SLOTS, 2)), dma((PEERS,)), dma((PEERS,)),
            dma((10, n_chunks)), dma((10, n_chunks)),
        ],
        compiler_params=pltpu.CompilerParams(collective_id=1, has_side_effects=True, vmem_limit_bytes=LIMIT),
    )(attended, tokens, normed, early, w_gate, w_up, w_out, w_down)


def solution(mesh):
    def local_step(tokens, lengths, k_cache, v_cache, norm_gain, w_query, w_key, w_value, w_out, w_gate, w_up, w_down):
        rows = tokens.shape[0] // PEERS
        q_all, key_new, value_new, normed, early = project_call(tokens, lengths, norm_gain, w_query, w_key, w_value, w_gate, w_up)
        attended, key_new, value_new = attend_call(lengths, q_all, key_new, value_new, k_cache, v_cache)
        y = combine_call(attended, tokens, normed, early, w_gate, w_up, w_out, w_down)
        return y, key_new.reshape(rows, 1, 128), value_new.reshape(rows, 1, 128)

    in_specs = (P('replica', None), P('replica'), P('replica', None, None, None), P('replica', None, None, None), P(None), P(None, 'model'), P(None, None), P(None, None), P('model', None), P(None, 'model'), P(None, 'model'), P('model', None))
    out_specs = (P('replica', None), P(('replica', 'model'), None, None), P(('replica', 'model'), None, None))
    return jax.shard_map(local_step, mesh=mesh, in_specs=in_specs, out_specs=out_specs, check_vma=False)
```

time: 127 us -> 102 us (0.80); the launches traced: 128 us -> 100 us
  Pallas kernels: 120 us -> 97.7 us
  local copies, waits for them, and re-layouts: 7.89 us -> 1.67 us
    pallas_call x3, Pallas kernels: 120 us -> 97.7 us  [the longest x1 66.9 us: combine_call(): pl.pallas_call(combine_kernel, name='combine', out_shape=pltpu.VMEM((batc...]
    unnamed x7 -> x3, local copies, waits for them, and re-layouts: 5.09 us -> 1.67 us
    reshape x2 -> x0, local copies, waits for them, and re-layouts: 2.8 us -> none  [the longest x1 1.47 us: local_step(): lengths.reshape(batch, 1)]
where the time goes in v2:
time: 102 us; the launch traced here: 100 us
  Pallas kernels  97.7 us (96%)
  local copies, waits for them, and re-layouts  1.67 us (2%)
    pallas_call x1, Pallas kernels, combine_call(): pl.pallas_call(combine_kernel, name='combine', out_shape=pltpu.VMEM((batc...  66.9 us
    pallas_call x1, Pallas kernels, project_call(): pl.pallas_call(project_kernel, name='project', out_shape=(pltpu.VMEM((wid...  16.6 us
    pallas_call x1, Pallas kernels, attend_call(): pl.pallas_call(attend_kernel, name='attend', out_shape=(pltpu.VMEM((heads...  14.3 us

profile of v2, /device:TPU:0, one launch (start us, length us, event | category | flops | bytes accessed | tf_op | source)
XLA Modules:
  0.0 100.1 jit_solution(11812685412687364679)
XLA Ops:
  0.6 0.0 copy-start
  0.6 16.6 %project.1 = (bf16[48,32,128]{2,1,0:T(8,128)(2,1)S(1)}, bf16[32,128]{1,0:T(8,128)(2,1)S(1)}, bf16[32,128]{1,0:T(8,128)(2,1)S(1)}, bf16[256,6144]{1,0:T(8,128)(2,1)S(1)}, bf16[256,1024]{1,0:T(8,128)(2,1)S(1)}) custom-call(bf16[256,6144]{1,0:T(8,128)(2,1)} %x_hbm.3, s32[256]{0:T(256)} %lengths_ref.1, bf16[6144]{0:T(1024)(128)(2,1)} %gain_hbm.1, ...), custom_call_target="tpu_custom_call" | custom-call | tf_op jit(solution)/shard_map/project/pallas_call | solution.py:500
  17.3 0.0 copy-done
  17.3 14.3 %attend.1 = (bf16[48,32,128]{2,1,0:T(8,128)(2,1)S(1)}, bf16[32,128]{1,0:T(8,128)(2,1)}, bf16[32,128]{1,0:T(8,128)(2,1)}) custom-call(s32[256]{0:T(256)S(1)} %copy-done, bf16[48,32,128]{2,1,0:T(8,128)(2,1)S(1)} %get-tuple-element.11.q_in, bf16[32,128]{1,0:T(8,128)(2,1)S(1)} %get-tuple-element.12.k16, bf16[32,128]{1,0:T(8,128)(2,1)S(1)} %get-tuple-element.13.v16, ...), custom_call_target="tpu_custom_call" | custom-call | tf_op jit(solution)/shard_map/attend/pallas_call | solution.py:531
  31.5 66.9 %combine.1 = bf16[256,6144]{1,0:T(8,128)(2,1)S(1)} custom-call(bf16[48,32,128]{2,1,0:T(8,128)(2,1)S(1)} %get-tuple-element.14.o_ref, bf16[256,6144]{1,0:T(8,128)(2,1)} %x_hbm.3, bf16[256,6144]{1,0:T(8,128)(2,1)S(1)} %get-tuple-element.15.normed, bf16[256,1024]{1,0:T(8,128)(2,1)S(1)} %get-tuple-element.16.early_ref, bf16[6144,3072]{1,0:T(8,128)(2,1)} %gate_hbm.3, ...), custom_call_target="tpu_custom_call" | custom-call | tf_op jit(solution)/shard_map/combine/pallas_call | solution.py:564
  98.4 1.7 %copy.16 = bf16[256,6144]{1,0:T(8,128)(2,1)} copy(bf16[256,6144]{1,0:T(8,128)(2,1)S(1)} %combine.1) | data formatting | bytes 6291456
Async XLA Ops:
  0.6 16.6 %copy-start = (s32[256]{0:T(256)S(1)}, s32[256]{0:T(256)}, u32[]{:S(2)}) copy-start(s32[256]{0:T(256)} %lengths_ref.1) | copy-start | bytes 3076

commit v3 on v2

--- a/solution.py
+++ b/solution.py
@@ -18,8 +18,12 @@
 BLOCK = 512
 EARLY = 4
 CHUNK = 512
-ITEMS = 4
-RING = 3
+ITEMS = 8
+PIECES = 12
+PIECE_STEP = 2
+AHEAD = 2
+C_SLOTS = 3
+RING = 4
 CHUNK_COLS = 512
 LAGS = (0, 1, 4, 10, 14, 18, 19)
 
@@ -175,9 +179,9 @@
         copy.wait()
 
 
-def attend_kernel(lengths_ref, q_in, k16, v16, k_hbm, v_hbm, o_ref, key_out, value_out,
-                  q_scr, o_scr, k_scr, v_scr, k_buf, v_buf, item_row, item_chunk, m_run, l_run, acc_run,
-                  k_sem, v_sem, out_sem):
+def attend_kernel(lengths_ref, q_in, k16, v16, k_hbm, v_hbm, gate_hbm, up_hbm, o_ref, key_out, value_out, ahead_ref,
+                  q_scr, o_scr, k_scr, v_scr, s_scr, top_scr, new_scr, k_buf, v_buf, item_row, item_chunk, m_run, l_run, acc_run,
+                  k_sem, v_sem, out_sem, a_sem):
     me = lax.axis_index("model")
     rows = o_ref.shape[1]
     head_count = o_ref.shape[0]
@@ -222,6 +226,23 @@
     for g in range(RING - 1):
         state = launch(g, state)
 
+    half = BLOCK // 2
+    ahead = []
+    for p in range(AHEAD):
+        columns = pl.ds((EARLY + p) * half, half)
+        ahead.append(pltpu.make_async_copy(gate_hbm.at[:, columns], ahead_ref.at[p, :, pl.ds(0, half)], a_sem.at[p, 0]))
+        ahead.append(pltpu.make_async_copy(up_hbm.at[:, columns], ahead_ref.at[p, :, pl.ds(half, half)], a_sem.at[p, 1]))
+    piece_rows = gate_hbm.shape[0] * AHEAD // PIECES
+
+    def piece(i):
+        @pl.when(i < PIECES)
+        def _():
+            p = lax.div(i, PIECES // AHEAD)
+            at = pl.ds(pl.multiple_of(lax.rem(i, PIECES // AHEAD) * piece_rows, piece_rows), piece_rows)
+            columns = pl.ds(pl.multiple_of((EARLY + p) * half, half), half)
+            pltpu.make_async_copy(gate_hbm.at[at, columns], ahead_ref.at[p, at, pl.ds(0, half)], a_sem.at[p, 0]).start()
+            pltpu.make_async_copy(up_hbm.at[at, columns], ahead_ref.at[p, at, pl.ds(half, half)], a_sem.at[p, 1]).start()
+
     outputs = [pltpu.make_async_copy(k16, key_out, out_sem.at[0]), pltpu.make_async_copy(v16, value_out, out_sem.at[1])]
     for copy in outputs:
         copy.start()
@@ -232,60 +253,82 @@
     l_run[...] = jnp.ones_like(l_run)
     acc_run[...] = jnp.zeros_like(acc_run)
 
-    def body(g, state):
-        state = launch(g + RING - 1, state)
-        for j in range(ITEMS):
-            for copy in copies(g, j):
-                copy.wait()
-        m, l, acc = m_run[...], l_run[...], acc_run[...]
+    def score(g):
+        side = lax.rem(g, 2)
         blank = jnp.zeros((head_count, 128), BF16)
-        scored = []
         for p in range(ITEMS // 2):
             slot = lax.rem(g, RING) * (ITEMS // 2) + p
-            news, q_rows = [], []
+            q_rows, lefts = [], []
             for j in range(2):
                 n = g * ITEMS + 2 * p + j
                 b, c = item_row[n], item_chunk[n]
                 q16 = q_scr[b]
-                q32 = q16.astype(F32)
                 q_rows.append(jnp.concatenate([q16, blank] if j == 0 else [blank, q16], axis=1))
-                s_new = jnp.sum(q32 * k_scr[pl.ds(b, 1), :], axis=-1, keepdims=True) * scale
-                news.append((b, c, s_new, lengths_ref[base + b] - c * CHUNK))
+                new_scr[side, 2 * p + j] = jnp.sum(q16.astype(F32) * k_scr[pl.ds(b, 1), :], axis=-1, keepdims=True) * scale
+                lefts.append(lengths_ref[base + b] - c * CHUNK)
             s_pair = lax.dot_general(jnp.concatenate(q_rows, axis=0), k_buf[slot], (((1,), (1,)), ((), ())), preferred_element_type=F32) * scale
             for j in range(2):
-                b, c, s_new, left = news[j]
                 s = s_pair[j * head_count:(j + 1) * head_count]
-                s = jnp.where(lax.broadcasted_iota(jnp.int32, s.shape, 1) < left, s, MASK_VALUE)
-                scored.append((s, jnp.max(s, axis=-1, keepdims=True), s_new, b, c))
+                s = jnp.where(lax.broadcasted_iota(jnp.int32, s.shape, 1) < lefts[j], s, MASK_VALUE)
+                s_scr[side, 2 * p + j] = s
+                top_scr[side, 2 * p + j] = jnp.max(s, axis=-1, keepdims=True)
+
+    def mix(g):
+        side = lax.rem(g, 2)
+        m, l, acc = m_run[...], l_run[...], acc_run[...]
         for p in range(ITEMS // 2):
             slot = lax.rem(g, RING) * (ITEMS // 2) + p
-            tops, weights, shrinks = [], [], []
+            weights, states = [], []
             for j in range(2):
-                s, s_max, s_new, b, c = scored[2 * p + j]
-                m_prev = jnp.where(c == 0, s_new, m)
-                m = jnp.maximum(m_prev, s_max)
-                e = jnp.exp(s - m)
+                n = g * ITEMS + 2 * p + j
+                b, c = item_row[n], item_chunk[n]
+                m_prev = jnp.where(c == 0, new_scr[side, 2 * p + j], m)
+                m = jnp.maximum(m_prev, top_scr[side, 2 * p + j])
+                e = jnp.exp(s_scr[side, 2 * p + j] - m)
                 shrink = jnp.exp(m_prev - m)
                 l = jnp.where(c == 0, 1.0, l) * shrink + jnp.sum(e, axis=-1, keepdims=True)
-                tops.append(l)
-                shrinks.append(shrink)
+                states.append((b, c, l, shrink))
                 weights.append(e.astype(BF16))
             mixed = jnp.dot(jnp.concatenate(weights, axis=0), v_buf[slot], preferred_element_type=F32)
-            for j in range(2):
-                _, _, _, b, c = scored[2 * p + j]
+            for j, (b, c, l_item, shrink) in enumerate(states):
                 part = mixed[j * head_count:(j + 1) * head_count, j * 128:(j + 1) * 128]
-                acc = jnp.where(c == 0, v_scr[pl.ds(b, 1), :], acc) * shrinks[j] + part
-                o_scr[b] = acc / tops[j]
+                acc = jnp.where(c == 0, v_scr[pl.ds(b, 1), :], acc) * shrink + part
+                o_scr[b] = acc / l_item
         m_run[...], l_run[...], acc_run[...] = m, l, acc
+
+    for j in range(ITEMS):
+        copies(0, j)[0].wait()
+    score(0)
+
+    def body(g, state):
+        state = launch(g + RING - 1, state)
+        for k in range(PIECE_STEP):
+            piece(g * PIECE_STEP + k)
+
+        @pl.when(g + 1 < bodies)
+        def _():
+            for j in range(ITEMS):
+                copies(g + 1, j)[0].wait()
+        for j in range(ITEMS):
+            copies(g, j)[1].wait()
+        mix(g)
+        score(g + 1)
         return state
 
     lax.fori_loop(0, bodies, body, state)
+
+    def rest(i, _):
+        piece(i)
+        return 0
+    lax.fori_loop(bodies * PIECE_STEP, PIECES, rest, 0)
+    for copy in ahead:
+        copy.wait()
     for copy in outputs:
         copy.wait()
     o_ref[...] = jnp.swapaxes(o_scr[...], 0, 1).astype(BF16)
 
 
-def combine_kernel(o_ref, x_hbm, normed, early_ref, gate_hbm, up_hbm, wo_hbm, wd_hbm, y_ref,
+def combine_kernel(o_ref, x_hbm, normed, early_ref, ahead_ref, gate_hbm, up_hbm, wo_hbm, wd_hbm, y_ref,
                    act, ring, o_full, x_rows, part, pair_in, in1x, in1y, in2x, in2y,
                    x_sem, sems, o_send, o_recv, c_send, c_recv):
     me = lax.axis_index("model")
@@ -297,7 +340,7 @@
     y_peer = me + 4 - 8 * yi
     batch = normed.shape[0]
     rows = batch // PEERS
-    late = gate_hbm.shape[1] // (BLOCK // 2) - EARLY
+    late = gate_hbm.shape[1] // (BLOCK // 2) - EARLY - AHEAD
     n_chunks = y_ref.shape[1] // CHUNK_COLS
     o_width = wo_hbm.shape[0]
     f_width = wd_hbm.shape[0]
@@ -307,7 +350,7 @@
     early_width = EARLY * half
 
     def gu(n, slot):
-        return gate_up_copies(n + EARLY, slot, gate_hbm, up_hbm, ring, sems)
+        return gate_up_copies(n + EARLY + AHEAD, slot, gate_hbm, up_hbm, ring, sems)
 
     def down(t, slot):
         columns = pl.ds(pl.multiple_of(t * CHUNK_COLS, CHUNK_COLS), CHUNK_COLS)
@@ -318,7 +361,7 @@
         )
 
     def fetch(n):
-        slot = lax.rem(n, SLOTS)
+        slot = lax.rem(n, C_SLOTS)
 
         @pl.when(n < late)
         def _():
@@ -330,7 +373,7 @@
             for copy in down(n - late, slot):
                 copy.start()
 
-    for copy in gu(0, 0):
+    for copy in gu(0, 0) + gu(1, 1):
         copy.start()
     row_x = core * 128 + xi * 32 + yi * 16
     row_y = core * 128 + 64 + yi * 32 + xi * 16
@@ -349,21 +392,21 @@
         sends[-1].start()
     o_full[:, mine, :] = o_ref[pl.ds(me * 6, 6)]
     act[:, o_width:o_width + early_width] = early_ref[...]
-    for copy in gu(1, 1):
-        copy.start()
+    for p in range(AHEAD):
+        at = o_width + early_width + p * half
+        act[:, at:at + half] = hidden_block(normed[...], ahead_ref[p])
+        if p == 0:
+            for copy in gu(2, 2):
+                copy.start()
+    early_width += AHEAD * half
 
     def block_step(n, _):
-        slot = lax.rem(n, SLOTS)
+        slot = lax.rem(n, C_SLOTS)
         for copy in gu(n, slot):
             copy.wait()
-
-        @pl.when(n == 0)
-        def _():
-            fetch(2)
-            fetch(3)
         at = pl.ds(pl.multiple_of(o_width + early_width + n * half, half), half)
         act[:, at] = hidden_block(normed[...], ring[slot])
-        fetch(n + SLOTS)
+        fetch(n + C_SLOTS)
         return 0
 
     lax.fori_loop(0, late - 1, block_step, 0)
@@ -429,12 +472,12 @@
             copy.wait_recv()
 
     def stage_compute(t):
-        slot = lax.rem(t + late, SLOTS)
+        slot = lax.rem(t + late, C_SLOTS)
         for copy in down(t, slot):
             copy.wait()
         part[t] = jnp.dot(act[...], ring[slot, pl.ds(0, o_width + f_width), pl.ds(0, CHUNK_COLS)], preferred_element_type=F32)
         pair_sum(t).start()
-        fetch(t + late + SLOTS)
+        fetch(t + late + C_SLOTS)
 
     def stage_scatter1(t):
         pair_sum(t).wait_recv()
@@ -525,7 +568,7 @@
     )(tokens, lengths, norm_gain, w_query, w_key, w_value, w_gate, w_up)
 
 
-def attend_call(lengths, q_all, key_new, value_new, k_cache, v_cache):
+def attend_call(lengths, q_all, key_new, value_new, k_cache, v_cache, w_gate, w_up):
     heads, rows, _ = q_all.shape
     dma = pltpu.SemaphoreType.DMA
     return pl.pallas_call(
@@ -535,14 +578,18 @@
             pltpu.VMEM((heads, rows, 128), BF16),
             jax.ShapeDtypeStruct((rows, 128), BF16),
             jax.ShapeDtypeStruct((rows, 128), BF16),
+            pltpu.VMEM((AHEAD, w_gate.shape[0], BLOCK), BF16),
         ),
-        in_specs=[SM, VM, VM, VM, ANY, ANY],
-        out_specs=(VM, ANY, ANY),
+        in_specs=[SM, VM, VM, VM, ANY, ANY, ANY, ANY],
+        out_specs=(VM, ANY, ANY, VM),
         scratch_shapes=[
             pltpu.VMEM((rows, heads, 128), BF16),
             pltpu.VMEM((rows, heads, 128), F32),
             pltpu.VMEM((rows, 128), F32),
             pltpu.VMEM((rows, 128), F32),
+            pltpu.VMEM((2, ITEMS, heads, CHUNK), F32),
+            pltpu.VMEM((2, ITEMS, heads, 1), F32),
+            pltpu.VMEM((2, ITEMS, heads, 1), F32),
             pltpu.VMEM((RING * ITEMS // 2, CHUNK, 256), BF16),
             pltpu.VMEM((RING * ITEMS // 2, CHUNK, 256), BF16),
             pltpu.SMEM((rows * (k_cache.shape[2] // CHUNK) + RING * ITEMS,), jnp.int32),
@@ -550,14 +597,14 @@
             pltpu.VMEM((heads, 1), F32),
             pltpu.VMEM((heads, 1), F32),
             pltpu.VMEM((heads, 128), F32),
-            dma((RING * ITEMS,)), dma((RING * ITEMS,)), dma((2,)),
+            dma((RING * ITEMS,)), dma((RING * ITEMS,)), dma((2,)), dma((AHEAD, 2)),
         ],
         compiler_params=pltpu.CompilerParams(vmem_limit_bytes=20 << 20),
-    )(lengths, q_all, key_new, value_new, k_cache, v_cache)
-
-
-def combine_call(attended, tokens, normed, early, w_gate, w_up, w_out, w_down):
-    attended, normed, early = (pltpu.with_memory_space_constraint(a, pltpu.VMEM) for a in (attended, normed, early))
+    )(lengths, q_all, key_new, value_new, k_cache, v_cache, w_gate, w_up)
+
+
+def combine_call(attended, tokens, normed, early, ahead, w_gate, w_up, w_out, w_down):
+    attended, normed, early, ahead = (pltpu.with_memory_space_constraint(a, pltpu.VMEM) for a in (attended, normed, early, ahead))
     batch, width = tokens.shape
     n_chunks = width // CHUNK_COLS
     dma = pltpu.SemaphoreType.DMA
@@ -565,11 +612,11 @@
         combine_kernel,
         name="combine",
         out_shape=pltpu.VMEM((batch, width), BF16),
-        in_specs=[VM, ANY, VM, VM, ANY, ANY, ANY, ANY],
+        in_specs=[VM, ANY, VM, VM, VM, ANY, ANY, ANY, ANY],
         out_specs=VM,
         scratch_shapes=[
             pltpu.VMEM((batch, w_out.shape[0] + w_down.shape[0]), BF16),
-            pltpu.VMEM((SLOTS, width, BLOCK), BF16),
+            pltpu.VMEM((C_SLOTS, width, BLOCK), BF16),
             pltpu.VMEM((6, batch, 128), BF16),
             pltpu.VMEM((2, 16, width), BF16),
             pltpu.VMEM((n_chunks, batch, CHUNK_COLS), F32),
@@ -578,19 +625,19 @@
             pltpu.VMEM((n_chunks, 32, CHUNK_COLS), F32),
             pltpu.VMEM((n_chunks, 16, CHUNK_COLS), F32),
             pltpu.VMEM((n_chunks, 16, CHUNK_COLS), F32),
-            dma((2,)), dma((SLOTS, 2)), dma((PEERS,)), dma((PEERS,)),
+            dma((2,)), dma((C_SLOTS, 2)), dma((PEERS,)), dma((PEERS,)),
             dma((10, n_chunks)), dma((10, n_chunks)),
         ],
-        compiler_params=pltpu.CompilerParams(collective_id=1, has_side_effects=True, vmem_limit_bytes=LIMIT),
-    )(attended, tokens, normed, early, w_gate, w_up, w_out, w_down)
+        compiler_params=pltpu.CompilerParams(collective_id=1, has_side_effects=True, vmem_limit_bytes=40 << 20),
+    )(attended, tokens, normed, early, ahead, w_gate, w_up, w_out, w_down)
 
 
 def solution(mesh):
     def local_step(tokens, lengths, k_cache, v_cache, norm_gain, w_query, w_key, w_value, w_out, w_gate, w_up, w_down):
         rows = tokens.shape[0] // PEERS
         q_all, key_new, value_new, normed, early = project_call(tokens, lengths, norm_gain, w_query, w_key, w_value, w_gate, w_up)
-        attended, key_new, value_new = attend_call(lengths, q_all, key_new, value_new, k_cache, v_cache)
-        y = combine_call(attended, tokens, normed, early, w_gate, w_up, w_out, w_down)
+        attended, key_new, value_new, ahead = attend_call(lengths, q_all, key_new, value_new, k_cache, v_cache, w_gate, w_up)
+        y = combine_call(attended, tokens, normed, early, ahead, w_gate, w_up, w_out, w_down)
         return y, key_new.reshape(rows, 1, 128), value_new.reshape(rows, 1, 128)
 
     in_specs = (P('replica', None), P('replica'), P('replica', None, None, None), P('replica', None, None, None), P(None), P(None, 'model'), P(None, None), P(None, None), P('model', None), P(None, 'model'), P(None, 'model'), P('model', None))

time: 102 us -> 94.6 us (0.927); the launches traced: 100 us -> 95.1 us
  Pallas kernels: 97.7 us -> 92.7 us
    pallas_call x1, Pallas kernels: 66.9 us -> 64 us  [combine_call(): pl.pallas_call(combine_kernel, name='combine', out_shape=pltpu.VMEM((batc...]
    pallas_call x1, Pallas kernels: 14.3 us -> 12.1 us  [attend_call(): pl.pallas_call(attend_kernel, name='attend', out_shape=(pltpu.VMEM((heads...]
where the time goes in v3:
time: 94.6 us; the launch traced here: 95.1 us
  Pallas kernels  92.7 us (98%)
  local copies, waits for them, and re-layouts  1.67 us (2%)
    pallas_call x1, Pallas kernels, combine_call(): pl.pallas_call(combine_kernel, name='combine', out_shape=pltpu.VMEM((batc...  64 us
    pallas_call x1, Pallas kernels, project_call(): pl.pallas_call(project_kernel, name='project', out_shape=(pltpu.VMEM((wid...  16.6 us
    pallas_call x1, Pallas kernels, attend_call(): pl.pallas_call(attend_kernel, name='attend', out_shape=(pltpu.VMEM((heads...  12.1 us

profile of v3, /device:TPU:0, one launch (start us, length us, event | category | flops | bytes accessed | tf_op | source)
XLA Modules:
  0.0 95.1 jit_solution(142031587066577877)
XLA Ops:
  0.6 0.0 copy-start
  0.6 16.6 %project.1 = (bf16[48,32,128]{2,1,0:T(8,128)(2,1)S(1)}, bf16[32,128]{1,0:T(8,128)(2,1)S(1)}, bf16[32,128]{1,0:T(8,128)(2,1)S(1)}, bf16[256,6144]{1,0:T(8,128)(2,1)S(1)}, bf16[256,1024]{1,0:T(8,128)(2,1)S(1)}) custom-call(bf16[256,6144]{1,0:T(8,128)(2,1)} %x_hbm.3, s32[256]{0:T(256)} %lengths_ref.1, bf16[6144]{0:T(1024)(128)(2,1)} %gain_hbm.1, ...), custom_call_target="tpu_custom_call" | custom-call | tf_op jit(solution)/shard_map/project/pallas_call | solution.py:543
  17.3 0.0 copy-done
  17.3 12.1 %attend.1 = (bf16[48,32,128]{2,1,0:T(8,128)(2,1)S(1)}, bf16[32,128]{1,0:T(8,128)(2,1)}, bf16[32,128]{1,0:T(8,128)(2,1)}, bf16[2,6144,512]{2,1,0:T(8,128)(2,1)S(1)}) custom-call(s32[256]{0:T(256)S(1)} %copy-done, bf16[48,32,128]{2,1,0:T(8,128)(2,1)S(1)} %get-tuple-element.12.q_in, bf16[32,128]{1,0:T(8,128)(2,1)S(1)} %get-tuple-element.13.k16, ...), custom_call_target="tpu_custom_call" | custom-call | tf_op jit(solution)/shard_map/attend/pallas_call | solution.py:574
  29.4 64.0 %combine.1 = bf16[256,6144]{1,0:T(8,128)(2,1)S(1)} custom-call(bf16[48,32,128]{2,1,0:T(8,128)(2,1)S(1)} %get-tuple-element.15.o_ref, bf16[256,6144]{1,0:T(8,128)(2,1)} %x_hbm.3, bf16[256,6144]{1,0:T(8,128)(2,1)S(1)} %get-tuple-element.16.normed, bf16[256,1024]{1,0:T(8,128)(2,1)S(1)} %get-tuple-element.17.early_ref, ...), custom_call_target="tpu_custom_call" | custom-call | tf_op jit(solution)/shard_map/combine/pallas_call | solution.py:611
  93.4 1.7 %copy.16 = bf16[256,6144]{1,0:T(8,128)(2,1)} copy(bf16[256,6144]{1,0:T(8,128)(2,1)S(1)} %combine.1) | data formatting | bytes 6291456
Async XLA Ops:
  0.6 16.6 %copy-start = (s32[256]{0:T(256)S(1)}, s32[256]{0:T(256)}, u32[]{:S(2)}) copy-start(s32[256]{0:T(256)} %lengths_ref.1) | copy-start | bytes 3076

commit v4 on v3

--- a/solution.py
+++ b/solution.py
@@ -23,7 +23,7 @@
 PIECE_STEP = 2
 AHEAD = 2
 C_SLOTS = 3
-RING = 4
+RING = 5
 CHUNK_COLS = 512
 LAGS = (0, 1, 4, 10, 14, 18, 19)
 
@@ -76,6 +76,9 @@
         pltpu.make_async_copy(wv_hbm, ring.at[1, :, pl.ds(384, 128)], sems.at[1, 2]),
     )
     gu = lambda block, slot: gate_up_copies(block, slot, gate_hbm, up_hbm, ring, sems)
+
+    for copy in first:
+        copy.start()
 
     hb = batch // 2
     l_copy.wait()
@@ -93,8 +96,6 @@
     sin_scr[hb:] = jnp.where(low, -sin_turn, sin_part)
 
     x_copy.wait()
-    for copy in first:
-        copy.start()
     tiles = width // 128
 
     def square_rows(r, _):
@@ -201,10 +202,14 @@
         start = pl.multiple_of(jnp.minimum(item_chunk[n] * CHUNK, context - CHUNK), CHUNK)
         row = base + item_row[n]
         slot = lax.rem(g, RING) * (ITEMS // 2) + j // 2
-        sem = lax.rem(g, RING) * ITEMS + j
+        sem = lax.rem(g, RING)
         src, lanes = pl.ds(start, CHUNK), pl.ds(128 * (j % 2), 128)
         return (pltpu.make_async_copy(k_hbm.at[row, 0, src, :], k_buf.at[slot, :, lanes], k_sem.at[sem]),
                 pltpu.make_async_copy(v_hbm.at[row, 0, src, :], v_buf.at[slot, :, lanes], v_sem.at[sem]))
+
+    def arrived(g, buf, sems):
+        at = buf.at[pl.ds(lax.rem(g, RING) * (ITEMS // 2), ITEMS // 2)]
+        pltpu.make_async_copy(at, at, sems.at[lax.rem(g, RING)]).wait()
 
     def launch(g, state):
         b, c = state
@@ -296,8 +301,7 @@
                 o_scr[b] = acc / l_item
         m_run[...], l_run[...], acc_run[...] = m, l, acc
 
-    for j in range(ITEMS):
-        copies(0, j)[0].wait()
+    arrived(0, k_buf, k_sem)
     score(0)
 
     def body(g, state):
@@ -307,10 +311,8 @@
 
         @pl.when(g + 1 < bodies)
         def _():
-            for j in range(ITEMS):
-                copies(g + 1, j)[0].wait()
-        for j in range(ITEMS):
-            copies(g, j)[1].wait()
+            arrived(g + 1, k_buf, k_sem)
+        arrived(g, v_buf, v_sem)
         mix(g)
         score(g + 1)
         return state
@@ -597,7 +599,7 @@
             pltpu.VMEM((heads, 1), F32),
             pltpu.VMEM((heads, 1), F32),
             pltpu.VMEM((heads, 128), F32),
-            dma((RING * ITEMS,)), dma((RING * ITEMS,)), dma((2,)), dma((AHEAD, 2)),
+            dma((RING,)), dma((RING,)), dma((2,)), dma((AHEAD, 2)),
         ],
         compiler_params=pltpu.CompilerParams(vmem_limit_bytes=20 << 20),
     )(lengths, q_all, key_new, value_new, k_cache, v_cache, w_gate, w_up)

time: 94.6 us -> 92.7 us (0.980)
  Pallas kernels: 92.7 us -> 90 us
    pallas_call x1, Pallas kernels: 12.1 us -> 9.39 us  [attend_call(): pl.pallas_call(attend_kernel, name='attend', out_shape=(pltpu.VMEM((heads...]
where the time goes in v4:
time: 92.7 us; the launch traced here: 92.3 us
  Pallas kernels  90 us (97%)
  local copies, waits for them, and re-layouts  1.67 us (2%)
    pallas_call x1, Pallas kernels, combine_call(): pl.pallas_call(combine_kernel, name='combine', out_shape=pltpu.VMEM((batc...  64.9 us
    pallas_call x1, Pallas kernels, project_call(): pl.pallas_call(project_kernel, name='project', out_shape=(pltpu.VMEM((wid...  15.7 us
    pallas_call x1, Pallas kernels, attend_call(): pl.pallas_call(attend_kernel, name='attend', out_shape=(pltpu.VMEM((heads...  9.39 us

profile of v4, /device:TPU:0, one launch (start us, length us, event | category | flops | bytes accessed | tf_op | source)
XLA Modules:
  0.0 92.3 jit_solution(5046144321324671404)
XLA Ops:
  0.6 0.0 copy-start
  0.6 15.7 %project.1 = (bf16[48,32,128]{2,1,0:T(8,128)(2,1)S(1)}, bf16[32,128]{1,0:T(8,128)(2,1)S(1)}, bf16[32,128]{1,0:T(8,128)(2,1)S(1)}, bf16[256,6144]{1,0:T(8,128)(2,1)S(1)}, bf16[256,1024]{1,0:T(8,128)(2,1)S(1)}) custom-call(bf16[256,6144]{1,0:T(8,128)(2,1)} %x_hbm.3, s32[256]{0:T(256)} %lengths_ref.1, bf16[6144]{0:T(1024)(128)(2,1)} %gain_hbm.1, ...), custom_call_target="tpu_custom_call" | custom-call | tf_op jit(solution)/shard_map/project/pallas_call | solution.py:545
  16.4 0.0 copy-done
  16.4 9.4 %attend.1 = (bf16[48,32,128]{2,1,0:T(8,128)(2,1)S(1)}, bf16[32,128]{1,0:T(8,128)(2,1)}, bf16[32,128]{1,0:T(8,128)(2,1)}, bf16[2,6144,512]{2,1,0:T(8,128)(2,1)S(1)}) custom-call(s32[256]{0:T(256)S(1)} %copy-done, bf16[48,32,128]{2,1,0:T(8,128)(2,1)S(1)} %get-tuple-element.12.q_in, bf16[32,128]{1,0:T(8,128)(2,1)S(1)} %get-tuple-element.13.k16, ...), custom_call_target="tpu_custom_call" | custom-call | tf_op jit(solution)/shard_map/attend/pallas_call | solution.py:576
  25.8 64.9 %combine.1 = bf16[256,6144]{1,0:T(8,128)(2,1)S(1)} custom-call(bf16[48,32,128]{2,1,0:T(8,128)(2,1)S(1)} %get-tuple-element.15.o_ref, bf16[256,6144]{1,0:T(8,128)(2,1)} %x_hbm.3, bf16[256,6144]{1,0:T(8,128)(2,1)S(1)} %get-tuple-element.16.normed, bf16[256,1024]{1,0:T(8,128)(2,1)S(1)} %get-tuple-element.17.early_ref, ...), custom_call_target="tpu_custom_call" | custom-call | tf_op jit(solution)/shard_map/combine/pallas_call | solution.py:613
  90.7 1.7 %copy.16 = bf16[256,6144]{1,0:T(8,128)(2,1)} copy(bf16[256,6144]{1,0:T(8,128)(2,1)S(1)} %combine.1) | data formatting | bytes 6291456
Async XLA Ops:
  0.6 15.7 %copy-start = (s32[256]{0:T(256)S(1)}, s32[256]{0:T(256)}, u32[]{:S(2)}) copy-start(s32[256]{0:T(256)} %lengths_ref.1) | copy-start | bytes 3076
